TPU v7x, 128 devices: a whole 4x4x4 slice. The times are simulated.
128 devices in a mesh: data: 1, model: 128 (over z, y, x, core).
Axes of the slice: x: 4, y: 4, z: 4, core: 2. Of those that a mesh axis runs over, the one named last changes fastest.
Arguments:
- hidden: bfloat16 [64, 4096], P('data')
- w_head: bfloat16 [4096, 32768], P(None, 'model')
- store_keys: bfloat16 [131072, 4096], P('model')
- store_tok: int32 [131072], P('model')
- range_bounds: int32 [128, 129], P('model')
- temperature: float32 [], replicated
- mix_weight: float32 [], replicated
Outputs:
- output: float32 [64, 32768], P('data', 'model')
All inputs are finite; a program needn't handle non-finite values.
Results may differ from a plain program's by a relative error of at most 0.001.
Values are sent between devices in bfloat16 or wider.
A program may use at most 1 GiB of HBM per device.

v0:
```python
import jax
import jax.numpy as jnp
from jax import lax
from jax.sharding import PartitionSpec as P


def solution(mesh):
    group_size = mesh.shape['model']

    def local_step(hidden, w_local, keys_local, tok_local, bounds_local, value_a11, mix_weight):
        store_rows = keys_local.shape[0]
        shard_width = w_local.shape[1]
        vocab_size = shard_width * group_size
        key_norm = jnp.einsum('nd,nd->n', keys_local, keys_local, preferred_element_type=jnp.float32)
        cross_dot = jnp.einsum('nd,bd->nb', keys_local, hidden, preferred_element_type=jnp.float32)
        scores = (2.0 * cross_dot - key_norm[:, None]) / value_a11
        row_max = lax.pmax(jnp.max(scores, axis=0), 'model')
        kernel = jnp.exp(scores - row_max[None, :])
        part_total = jnp.sum(kernel, axis=0)
        owner = tok_local // shard_width
        bounds = bounds_local[0]
        positions = jnp.arange(store_rows, dtype=tok_local.dtype)
        counted = (positions >= bounds[owner]) & (positions < bounds[owner + 1])
        segment = jnp.where(counted, tok_local, vocab_size)
        part_hist = jax.ops.segment_sum(kernel, segment, num_segments=vocab_size)
        hist_local = lax.psum_scatter(part_hist, 'model', scatter_dimension=0, tiled=True)
        knn_total = lax.psum(part_total, 'model')
        logits = jnp.einsum('dv,bd->vb', w_local, hidden, preferred_element_type=jnp.float32)
        lm_max = lax.pmax(jnp.max(logits, axis=0), 'model')
        lm_exp = jnp.exp(logits - lm_max[None, :])
        lm_total = lax.psum(jnp.sum(lm_exp, axis=0), 'model')
        mixture = mix_weight * (hist_local / knn_total[None, :]) + (1.0 - mix_weight) * (lm_exp / lm_total[None, :])
        return jnp.log(mixture).T

    return jax.shard_map(local_step, mesh=mesh,
                         in_specs=(P('data', None), P(None, 'model'), P('model', None), P('model'),
                                   P('model', None), P(), P()),
                         out_specs=P('data', 'model'), check_vma=False)
```

profile of v0, /device:TPU:1, one launch (start us, length us, event | category | flops | bytes accessed | tf_op | source)
XLA Modules:
  0.0 782.4 jit_solution(16401262623505120836)
XLA Ops:
  6.5 0.0 copy-start
  6.5 0.0 reduce-scatter.2.cloned.1.call-start
  6.5 0.8 fusion.8
  7.4 0.0 copy-start.1
  7.4 6.2 gather_fusion
  13.6 6.2 gather_fusion.1
  20.5 5.1 fusion
  25.5 0.0 copy-done
  25.5 0.0 copy-done.1
  25.6 0.0 copy-start.2
  25.6 0.6 fusion.14
  26.1 6.2 fusion.13
  32.3 68.7 %all-reduce.1 = (f32[64]{0:T(128)S(1)}, f32[64]{0:T(128)S(1)}) all-reduce(f32[64]{0:T(128)S(1)} %get-tuple-element.13, f32[64]{0:T(128)S(1)} %get-tuple-element.15), channel_id=1, replica_groups=mesh['data'=1,'model'=128] {'model'}, use_global_device_ids=true, to_apply=%region_1.0 | all-reduce | flops 128 | bytes 1024 | tf_op jit(solution)/shard_map/pmax | solution.py:17
  101.0 0.2 fusion.12
  101.2 0.2 copy.8
  101.4 0.0 copy-done.2
  101.4 12.8 %scatter_custom_fusion = f32[32768,64]{1,0:T(8,128)} fusion(s32[1024]{0:T(1024)S(1)} %fusion.10, f32[1024,64]{1,0:T(8,128)S(1)} %copy.8, f32[]{:T(128)} %constant.9.clone.1), kind=kCustom, calls=%fused_computation.5 | custom fusion | flops 65536 | bytes 8388612 | tf_op jit(solution)/shard_map/scatter-add | solution.py:25
  114.2 12.7 %copy.9 = f32[32768,64]{0,1:T(8,128)} copy(f32[32768,64]{1,0:T(8,128)} %scatter_custom_fusion) | data formatting | bytes 16777216 | tf_op jit(solution)/shard_map/scatter-add | solution.py:25
  126.9 0.0 reduce-scatter.2.cloned.1.call-update
  127.5 0.2 fusion.5
  127.7 63.0 %all-reduce = (f32[64]{0:T(128)S(1)}, f32[64]{0:T(128)S(1)}) all-reduce(f32[64]{0:T(128)S(1)} %fusion.5, f32[64]{0:T(128)S(1)} %get-tuple-element.9), channel_id=1, replica_groups=mesh['data'=1,'model'=128] {'model'}, use_global_device_ids=true, to_apply=%region_9.10 | all-reduce | flops 128 | bytes 1024 | tf_op jit(solution)/shard_map/psum | solution.py:31
  190.7 583.3 %reduce-scatter.2.cloned.1.call-done = f32[256,64]{0,1:T(8,128)} async-done(((f32[32768,64]{0,1:T(8,128)}), f32[256,64]{0,1:T(8,128)}) %reduce-scatter.2.cloned.1.call-update) | async-done | bytes 65552 | tf_op jit(solution)/shard_map/reduce_scatter | solution.py:26
  774.0 1.6 log_bitcast_fusion
  (1 shorter events, 0.0 us)
Async XLA Ops:
  6.5 19.0 %copy-start = (bf16[4096,256]{1,0:T(8,128)(2,1)S(1)}, bf16[4096,256]{1,0:T(8,128)(2,1)}, u32[]{:S(2)}) copy-start(bf16[4096,256]{1,0:T(8,128)(2,1)} %param.8) | copy-start | bytes 6291460
  6.5 767.4 %reduce-scatter.2.cloned.1.call-start = ((), (), s32[]{:S(2)}) async-start(), calls=%async_computation.1 | async-start | bytes 8454144 | tf_op jit(solution)/shard_map/reduce_scatter | solution.py:26
  7.4 18.2 %copy-start.1 = (bf16[64,4096]{1,0:T(8,128)(2,1)S(1)}, bf16[64,4096]{1,0:T(8,128)(2,1)}, u32[]{:S(2)}) copy-start(bf16[64,4096]{1,0:T(8,128)(2,1)} %param.7) | copy-start | bytes 1572868
  25.6 75.8 %copy-start.2 = (s32[1024]{0:T(1024)S(1)}, s32[1024]{0:T(1024)}, u32[]{:S(2)}) copy-start(s32[1024]{0:T(1024)} %param.10) | copy-start | bytes 12292
Sparse Core Ops, SparseCore 0:
  127.0 646.9 reduce-scatter.1
where the time goes:
time: 789 us; the launch traced here: 782 us
  waiting for transfers between devices  583 us (74%)
  blocking collectives  132 us (17%)
  local copies, waits for them, and re-layouts  25.3 us (3%)
  other arithmetic  20.7 us (3%)
  between operations  14.8 us (2%)
    reduce_scatter x1, waiting for transfers between devices, local_step(): lax.psum_scatter(part_hist, 'model', scatter_dimension=0, tiled=True)  583 us
    pmax x1, blocking collectives, local_step(): row_max = lax.pmax(jnp.max(scores, axis=0), 'model')  68.7 us
    psum x1, blocking collectives, local_step(): lm_total = lax.psum(jnp.sum(lm_exp, axis=0), 'model')  63 us
  transfers between devices with their start and end apart: 1, of which 1 were waited for; matrix products, arithmetic and copies ran while one was open for 0% of the time, Pallas kernels for 0%

commit v1 on v0

v1 whole, which is shorter than its diff:
```python
import functools

import jax
import jax.numpy as jnp
from jax import lax
from jax.experimental import pallas as pl
from jax.experimental.pallas import tpu as pltpu
from jax.sharding import PartitionSpec as P

F32, BF16, I32 = jnp.float32, jnp.bfloat16, jnp.int32
SLOT_AXIS = (0, 1, 2, 0)
LN, EN = 128, 1024
NT = (((1,), (1,)), ((), ()))


def iota(shape, axis):
    return lax.broadcasted_iota(I32, shape, axis)


def coordinates(n):
    device = lax.axis_index('model')
    return device, device % 2, (device // 2) % n, (device // (2 * n)) % n, device // (2 * n * n)


def local_kernel(n, tok_ref, bounds_ref, tau_ref, hid_hbm, w_hbm, keys_hbm, rows_out, logits_out, tab_out,
                 hid, w, keys, score, dedup, onehot, lohot, e3, in_sem, key_sem):
    inner = 2 * n * n
    _, _, cx, cy, cz = coordinates(n)
    in_copies = (pltpu.make_async_copy(hid_hbm, hid, in_sem.at[0]), pltpu.make_async_copy(w_hbm, w, in_sem.at[1]))
    for c in in_copies:
        c.start()
    kchunk = LN
    nk = keys.shape[0] // kchunk

    def key_copy(c):
        rows = pl.ds(c * kchunk, kchunk)
        return pltpu.make_async_copy(keys_hbm.at[rows], keys.at[rows], key_sem.at[c])

    for c in range(nk):
        key_copy(c).start()

    lane = iota((8, LN), 1)
    sub = iota((8, LN), 0)
    pos = sub * LN + lane

    def prev(a):
        r = pltpu.roll(a, 1, 1)
        return jnp.where(lane == 0, pltpu.roll(r, 1, 0), r)

    tok = tok_ref[...]
    first = ((tok != prev(tok)) | (pos == 0)).astype(I32)
    c = first
    for sh in (1, 2, 4, 8, 16, 32, 64):
        c = c + jnp.where(lane >= sh, pltpu.roll(c, sh, 1), 0)
    tot = jnp.broadcast_to(c[:, 127:LN], (8, LN))
    acc = tot
    for sh in (1, 2, 4):
        acc = acc + jnp.where(sub >= sh, pltpu.roll(acc, sh, 0), 0)
    rank = c + acc - tot - 1

    owner = tok // 256
    bnd = bounds_ref[...]
    nb = bnd.shape[1] - 1
    lo_b = jnp.broadcast_to(bnd[:, :nb], (8, nb))
    hi_b = jnp.broadcast_to(bnd[:, 1:], (8, nb))
    if nb < LN:
        lo_b = jnp.concatenate([lo_b, jnp.zeros((8, LN - nb), I32)], axis=1)
        hi_b = jnp.concatenate([hi_b, jnp.zeros((8, LN - nb), I32)], axis=1)
    counted = (pos >= jnp.take_along_axis(lo_b, owner, axis=1)) & (pos < jnp.take_along_axis(hi_b, owner, axis=1))
    rank_d = jnp.where(counted, rank, -1)
    for t in range(8):
        rows = iota((EN, LN), 0)
        dedup[:, t * LN:(t + 1) * LN] = jnp.where(rank_d[t:t + 1, :] == rows, 1.0, 0.0).astype(BF16)

    h = tok // LN
    tile_first = ((h != prev(h)) | (pos == 0)).astype(I32)
    half = h % 2
    jc = owner % 2
    jp = ((owner // 2) % n, (owner // (2 * n)) % n, owner // (2 * n * n))
    lo = tok % LN
    val = (first * (rank % LN + 1) * (1 + 255 * half)).astype(F32)
    starts = [(tile_first * jnp.where(half == hf, part, 0)).astype(F32)
              for hf in range(2) for part in (rank // LN, rank % LN)]
    sub32 = iota((32, LN), 0)
    for t in range(8):
        cols = slice(t * LN, (t + 1) * LN)
        r = slice(t, t + 1)
        lohot[0:LN, cols] = jnp.where(lo[r, :] == iota((LN, LN), 0), val[r, :], 0.0).astype(BF16)
        lohot[LN:160, cols] = jnp.where(
            sub32 < 8, starts[0][r, :], jnp.where(sub32 < 16, starts[1][r, :], jnp.where(
                sub32 < 24, starts[2][r, :], starts[3][r, :]))).astype(BF16)
    coord = (cx, cy, cz)
    for a, (b2, b3) in enumerate(((2, 1), (2, 0), (1, 0))):
        row = ((jp[a] - coord[a] + n) % n) * inner + jp[b2] * (2 * n) + jp[b3] * 2 + jc
        for t in range(8):
            onehot[:, t * LN:(t + 1) * LN] = jnp.where(
                row[t:t + 1, :] == iota((LN, LN), 0), 1.0, 0.0).astype(BF16)
        tb = lax.dot_general(onehot[...], lohot[0:LN, :], NT, preferred_element_type=F32).astype(I32)
        us = lax.dot_general(lohot[LN:160, :], onehot[...], NT, preferred_element_type=F32).astype(I32)
        for d in range(n):
            tab_out[a, d, 0:inner, :] = tb[d * inner:(d + 1) * inner, :]
            for hf in range(2):
                tab_out[a, d, inner + hf:inner + hf + 1, :] = us[16 * hf:16 * hf + 1] * LN + us[16 * hf + 8:16 * hf + 9]

    for c in in_copies:
        c.wait()
    lg = jnp.dot(hid[...], w[...], preferred_element_type=F32)
    logits_out[...] = lg
    lm = jnp.max(lg, axis=1, keepdims=True)
    lz = jnp.sum(jnp.exp(lg - lm), axis=1, keepdims=True)

    tau = tau_ref[0]

    def score_step(c, carry):
        key_copy(2 * c).wait()
        key_copy(2 * c + 1).wait()
        rows = pl.ds(c * 256, 256)
        cross = lax.dot_general(hid[...], keys[rows, :], NT, preferred_element_type=F32)
        sq = jnp.zeros((256, LN), F32)
        for t in range(keys.shape[1] // LN):
            k = keys[rows, t * LN:(t + 1) * LN].astype(F32)
            sq = sq + k * k
        norm = jnp.sum(sq.T, axis=0, keepdims=True)
        sc = (2.0 * cross - norm) / tau
        score[2 * c] = sc[:, :LN]
        score[2 * c + 1] = sc[:, LN:]
        return carry

    lax.fori_loop(0, nk // 2, score_step, 0)

    sc = [score[t] for t in range(8)]
    m = jnp.max(functools.reduce(jnp.maximum, sc), axis=1, keepdims=True)
    z = jnp.zeros((64, LN), F32)
    for t in range(8):
        e = jnp.exp(sc[t] - m)
        z = z + e
        hi = e.astype(BF16)
        r1 = e - hi.astype(F32)
        mid = r1.astype(BF16)
        low = (r1 - mid.astype(F32)).astype(BF16)
        cols = slice(t * LN, (t + 1) * LN)
        e3[0:64, cols] = hi
        e3[64:LN, cols] = mid
        e3[LN:192, cols] = low
    z = jnp.sum(z, axis=1, keepdims=True)
    l64 = iota((64, LN), 1)
    stat = jnp.where(l64 == 0, m, jnp.where(l64 == 1, z, jnp.where(l64 == 2, lm, lz)))
    for q in range(8):
        rows_out[q // 4, q % 4, 8] = stat[q * 8:(q + 1) * 8, :]
    for c in range(4):
        dd = lax.dot_general(e3[...], dedup[c * 256:(c + 1) * 256, :], NT, preferred_element_type=F32)
        eu = dd[0:64] + (dd[64:LN] + dd[LN:192])
        for q in range(8):
            rows_out[q // 4, q % 4, 2 * c] = eu[q * 8:(q + 1) * 8, :LN]
            rows_out[q // 4, q % 4, 2 * c + 1] = eu[q * 8:(q + 1) * 8, LN:]


def exchange_kernel(n, own_rows, logits, own_tab, lam_ref, out_ref,
                    tab_pair, tab, tab_smem, lists0, lists1, lists2, lists3, part2, recv2, part3, recv3, fin, fin_in,
                    swap_sem, tab_send, tab_recv, smem_sem,
                    send1, recv1, send2, recv2_sem, send3, recv3_sem, fin_sem):
    inner = 2 * n * n
    block = 4 * n
    device, core, cx, cy, cz = coordinates(n)
    other = 1 - core
    partner = device + 1 - 2 * core
    coord = (cx + core * (cy - cx), cy + core * (cx - cy), cz)
    stride = (2 + core * (2 * n - 2), 2 * n + core * (2 - 2 * n), 2 * n * n)
    pcoord, pstride = (cx, cy, cz), (2, 2 * n, 2 * n * n)
    axis_of = (core, 1 - core, 2)
    row_stride = ((2, 2 * n), (2 * n, 2), (2 + core * (2 * n - 2), 2 * n + core * (2 - 2 * n)))

    def peer(v, d):
        return device + stride[v] * ((coord[v] + d) % n - coord[v])

    def remote(src, dst, ssem, rsem, dev):
        return pltpu.make_async_remote_copy(src_ref=src, dst_ref=dst, send_sem=ssem, recv_sem=rsem,
                                            device_id={'model': dev}, device_id_type=pl.DeviceIdType.MESH)

    lists = (lists0, lists1, lists2, lists3)
    far_first = sorted(range(1, n), key=lambda d: -min(d, n - d))
    lane = iota((8, LN), 1)

    barrier = pltpu.get_barrier_semaphore()
    partners = [partner] + [peer(v, d) for v in range(3) for d in range(1, n)]
    for p in partners:
        pl.semaphore_signal(barrier, inc=1, device_id={'model': p}, device_id_type=pl.DeviceIdType.MESH)
    pl.semaphore_wait(barrier, len(partners))

    tab_swap = remote(own_tab, tab_pair, swap_sem.at[0, 4], swap_sem.at[1, 4], partner)
    tab_swap.start()
    swaps = [remote(own_rows.at[other, s], lists[s].at[0], swap_sem.at[0, s], swap_sem.at[1, s], partner)
             for s in range(4)]
    for c in swaps:
        c.start()

    def tab_copy(a, d, l):
        src = own_tab if l == 0 else tab_pair
        return remote(src.at[a, d], tab.at[a, n - d - 1, l], tab_send.at[a, d - 1, l], tab_recv.at[a, n - d - 1, l],
                      device + pstride[a] * ((pcoord[a] + d) % n - pcoord[a]))

    def copy1(s, d, l):
        src = own_rows.at[core, s] if l == 0 else lists[s].at[0]
        return remote(src, lists[s].at[2 * (n - d) - 1 + l], send1.at[s, d - 1, l], recv1.at[s, n - d - 1, l],
                      peer(SLOT_AXIS[s], d))

    for d in far_first:
        for a in range(3):
            tab_copy(a, d, 0).start()
    for d in far_first:
        for s in range(4):
            copy1(s, d, 0).start()
    tab_swap.wait_recv()
    for d in far_first:
        for a in range(3):
            tab_copy(a, d, 1).start()
    for s in range(4):
        swaps[s].wait_recv()
        for d in far_first:
            copy1(s, d, 1).start()

    def tab_of(a, k, l):
        if k:
            return tab.at[a, k - 1, l]
        return (tab_pair if l else own_tab).at[a, 0]

    def list_of(s, k, l):
        if k == 0 and l == 0:
            return own_rows.at[core, s]
        return lists[s].at[2 * k - 1 + l]

    for d in range(1, n):
        for a in range(3):
            for l in range(2):
                tab_copy(a, d, l).wait_recv()
    smem_copies = [pltpu.make_async_copy(tab_of(a, k, l).at[pl.ds(inner, 2)], tab_smem.at[a, k, l], smem_sem.at[a, k, l])
                   for a in range(3) for k in range(n) for l in range(2)]
    for c in smem_copies:
        c.start()
    for c in smem_copies:
        c.wait()

    def stats(tiles):
        ms = [jnp.broadcast_to(t[:, 0:1], (8, LN)) for t in tiles]
        ls = [jnp.broadcast_to(t[:, 2:3], (8, LN)) for t in tiles]
        mm = functools.reduce(jnp.maximum, ms)
        ll = functools.reduce(jnp.maximum, ls)
        fs = [jnp.exp(a - mm) for a in ms]
        gs = [jnp.exp(a - ll) for a in ls]
        zz = sum(f * t[:, 1:2] for f, t in zip(fs, tiles))
        lzz = sum(g * t[:, 3:4] for g, t in zip(gs, tiles))
        return fs, jnp.where(lane == 0, mm, jnp.where(lane == 1, zz, jnp.where(lane == 2, ll, lzz)))

    def copy2(s, d):
        return remote(part2.at[s, d], recv2.at[s, n - d - 1], send2.at[s, d - 1], recv2_sem.at[s, n - d - 1],
                      peer((SLOT_AXIS[s] + 1) % 3, d))

    def copy3(s, d):
        return remote(part3.at[s, d], recv3.at[s, n - d - 1], send3.at[s, d - 1], recv3_sem.at[s, n - d - 1],
                      peer((SLOT_AXIS[s] + 2) % 3, d))

    src = [(k, l) for k in range(n) for l in range(2)]
    for s in range(4):
        v = SLOT_AXIS[s]
        a = axis_of[v]
        c2, c3 = coord[(v + 1) % 3], coord[(v + 2) % 3]
        s2, s3 = row_stride[v]
        for d in range(1, n):
            for l in range(2):
                copy1(s, d, l).wait_recv()
        fs, stat_tile = stats([list_of(s, k, l)[8] for k, l in src])
        for d2 in far_first + [0]:
            a2 = (c2 + d2) % n

            def pair_step(q, carry, s=s, a=a, a2=a2, c3=c3, s2=s2, s3=s3, d2=d2, fs=fs):
                row = a2 * s2 + ((c3 + q // 2) % n) * s3 + q % 2
                acc = [jnp.zeros((8, LN), F32)] * 2
                for i, (k, l) in enumerate(src):
                    entries = list_of(s, k, l)
                    packed = jnp.broadcast_to(tab_of(a, k, l)[pl.ds(row, 1), :], (8, LN))
                    for hf in range(2):
                        u = tab_smem[a, k, l, hf, ((n - k) % n) * inner + row]
                        kt = u // LN
                        merged = jnp.where(lane >= u % LN, entries[kt], entries[kt + 1])
                        idx = packed // 256 if hf else packed % 256
                        got = jnp.take_along_axis(merged, jnp.maximum(idx - 1, 0), axis=1)
                        acc[hf] = acc[hf] + jnp.where(idx > 0, got, 0.0) * fs[i]
                part2[s, d2, 2 * q] = acc[0]
                part2[s, d2, 2 * q + 1] = acc[1]
                return carry

            lax.fori_loop(0, 2 * n, pair_step, 0)
            part2[s, d2, block] = stat_tile
            if d2:
                copy2(s, d2).start()

    for s in range(4):
        for d in range(1, n):
            copy2(s, d).wait_recv()
        parts = [part2.at[s, 0]] + [recv2.at[s, k] for k in range(n - 1)]
        fs, stat_tile = stats([p[block] for p in parts])
        for d3 in far_first + [0]:
            for ch in range(4):
                part3[s, d3, ch] = sum(f * p[d3 * 4 + ch] for f, p in zip(fs, parts))
            part3[s, d3, 4] = stat_tile
            if d3:
                copy3(s, d3).start()

    for s in range(4):
        for d in range(1, n):
            copy3(s, d).wait_recv()
        parts = [part3.at[s, 0]] + [recv3.at[s, k] for k in range(n - 1)]
        fs, stat_tile = stats([p[4] for p in parts])
        for ch in range(4):
            fin[ch // 2, s, ch % 2] = sum(f * p[ch] for f, p in zip(fs, parts))
        for c in range(2):
            fin[c, s, 2] = stat_tile

    back = remote(fin.at[other], fin_in, fin_sem.at[0], fin_sem.at[1], partner)
    back.start()
    lam = lam_ref[0]

    def finish(block_ref, rows_half):
        for s in range(4):
            st = block_ref[s, 2]
            zz, ll, lzz = st[:, 1:2], st[:, 2:3], st[:, 3:4]
            rows = pl.ds(pl.multiple_of(rows_half * 32 + s * 8, 8), 8)
            for hf in range(2):
                cols = slice(hf * LN, (hf + 1) * LN)
                lm_exp = jnp.exp(logits[rows, cols] - ll)
                out_ref[rows, cols] = jnp.log(lam * (block_ref[s, hf] / zz) + (1.0 - lam) * (lm_exp / lzz))

    finish(fin.at[core], core)
    back.wait_recv()
    finish(fin_in, other)

    tab_swap.wait_send()
    for c in swaps:
        c.wait_send()
    back.wait_send()
    for d in range(1, n):
        for l in range(2):
            for a in range(3):
                tab_copy(a, d, l).wait_send()
            for s in range(4):
                copy1(s, d, l).wait_send()
        for s in range(4):
            copy2(s, d).wait_send()
            copy3(s, d).wait_send()


def step(n, hidden, w_local, keys_local, tok_local, bounds_local, tau, lam):
    tab_rows = 2 * n * n + 8
    block = 4 * n
    dim = hidden.shape[1]
    V, DMA = pltpu.VMEM, pltpu.SemaphoreType.DMA
    vm = pl.BlockSpec(memory_space=pltpu.VMEM)
    sm = pl.BlockSpec(memory_space=pltpu.SMEM)
    hbm = pl.BlockSpec(memory_space=pl.ANY)
    rows, logits, tab = pl.pallas_call(
        functools.partial(local_kernel, n),
        out_shape=(jax.ShapeDtypeStruct((2, 4, 9, 8, LN), F32), jax.ShapeDtypeStruct((64, 256), F32),
                   jax.ShapeDtypeStruct((3, n, tab_rows, LN), I32)),
        in_specs=[vm, vm, sm, hbm, hbm, hbm],
        out_specs=(vm, vm, vm),
        scratch_shapes=[
            V((64, dim), BF16), V((dim, 256), BF16), V((EN, dim), BF16), V((8, 64, LN), F32),
            V((EN, EN), BF16), V((LN, EN), BF16), V((160, EN), BF16), V((192, EN), BF16),
            DMA((2,)), DMA((8,))],
        name='local_scores',
    )(tok_local.reshape(8, LN), bounds_local, tau.reshape(1), hidden, w_local, keys_local)
    return pl.pallas_call(
        functools.partial(exchange_kernel, n),
        out_shape=jax.ShapeDtypeStruct((64, 256), F32),
        in_specs=[vm, vm, vm, sm],
        out_specs=vm,
        scratch_shapes=[
            V((3, n, tab_rows, LN), I32), V((3, n - 1, 2, tab_rows, LN), I32), pltpu.SMEM((3, n, 2, 2, LN), I32),
            *[V((2 * n - 1, 9, 8, LN), F32)] * 4, V((4, n, block + 1, 8, LN), F32), V((4, n - 1, block + 1, 8, LN), F32),
            V((4, n, 5, 8, LN), F32), V((4, n - 1, 5, 8, LN), F32), V((2, 4, 3, 8, LN), F32), V((4, 3, 8, LN), F32),
            DMA((2, 5)), DMA((3, n - 1, 2)), DMA((3, n - 1, 2)), DMA((3, n, 2)),
            DMA((4, n - 1, 2)), DMA((4, n - 1, 2)), DMA((4, n - 1)), DMA((4, n - 1)), DMA((4, n - 1)), DMA((4, n - 1)),
            DMA((2,))],
        compiler_params=pltpu.CompilerParams(collective_id=0, has_side_effects=True),
        name='exchange',
    )(rows, logits, tab, lam.reshape(1))


def solution(mesh):
    n = round((mesh.shape['model'] // 2) ** (1 / 3))
    return jax.shard_map(functools.partial(step, n), mesh=mesh,
                         in_specs=(P('data', None), P(None, 'model'), P('model', None), P('model'),
                                   P('model', None), P(), P()),
                         out_specs=P('data', 'model'), check_vma=False)
```

time: 789 us -> 65.1 us (0.08)
  waiting for transfers between devices: 583 us -> 0 us
  blocking collectives: 132 us -> 0 us
  Pallas kernels: 0 us -> 62 us
  local copies, waits for them, and re-layouts: 25.3 us -> 1.47 us
  other arithmetic: 20.7 us -> 0 us
  between operations: 14.8 us -> 1.31 us
    reduce_scatter x1 -> x0, waiting for transfers between devices: 583 us -> none  [local_step(): lax.psum_scatter(part_hist, 'model', scatter_dimension=0, tiled=True)]
    pmax x1 -> x0, blocking collectives: 68.7 us -> none  [local_step(): row_max = lax.pmax(jnp.max(scores, axis=0), 'model')]
    psum x1 -> x0, blocking collectives: 63 us -> none  [local_step(): lm_total = lax.psum(jnp.sum(lm_exp, axis=0), 'model')]
    pallas_call x0 -> x2, Pallas kernels: none -> 62 us  [the longest x1 50.4 us: step(): pl.pallas_call(functools.partial(exchange_kernel, n), out_shape=jax.Shape...]
    scatter-add x1 -> x0, other arithmetic: 12.8 us -> none  [local_step(): part_hist = jax.ops.segment_sum(kernel, segment, num_segments=vocab_size)]
    scatter-add x1 -> x0, local copies, waits for them, and re-layouts: 12.7 us -> none  [local_step(): part_hist = jax.ops.segment_sum(kernel, segment, num_segments=vocab_size)]
    gather x2 -> x0, local copies, waits for them, and re-layouts: 12.4 us -> none  [local_step(): counted = (positions >= bounds[owner]) & (positions < bounds[owner + 1])]
  transfers between devices with their start and end apart: 1 -> 0, of which waited for: 1 -> 0; matrix products, arithmetic and copies ran while one was open for 0% -> 0% of each run, Pallas kernels for 0% -> 0%
where the time goes in v1:
time: 65.1 us; the launch traced here: 64.8 us
  Pallas kernels  62 us (95%)
  local copies, waits for them, and re-layouts  1.47 us (2%)
  between operations  1.31 us (2%)
    pallas_call x1, Pallas kernels, step(): pl.pallas_call(functools.partial(exchange_kernel, n), out_shape=jax.Shape...  50.4 us
    pallas_call x1, Pallas kernels, step(): pl.pallas_call(functools.partial(local_kernel, n), out_shape=(jax.ShapeDt...  11.7 us
    unnamed x1, local copies, waits for them, and re-layouts  1.47 us

profile of v1, /device:TPU:1, one launch (start us, length us, event | category | flops | bytes accessed | tf_op | source)
XLA Modules:
  0.0 64.8 jit_solution(14517460098206503206)
XLA Ops:
  1.3 11.7 %local_scores.1 = (f32[2,4,9,8,128]{4,3,2,1,0:T(8,128)}, f32[64,256]{1,0:T(8,128)}, s32[3,4,40,128]{3,2,1,0:T(8,128)}) custom-call(s32[8,128]{1,0:T(8,128)} %bitcast.5, s32[1,129]{1,0:T(1,128)} %bounds_ref.1, f32[1]{0:T(128)} %bitcast.3.tau_ref, bf16[64,4096]{1,0:T(8,128)(2,1)} %hid_hbm.1, bf16[4096,256]{1,0:T(8,128)(2,1)} %w_hbm.1, bf16[1024,4096]{1,0:T(8,128)(2,1)} %keys_hbm.1), custom_call_target="tpu_custom_call" | custom-call | tf_op jit(solution)/shard_map/local_scores/pallas_call | solution.py:360
  13.0 50.4 %exchange.1 = f32[64,256]{1,0:T(8,128)} custom-call(f32[2,4,9,8,128]{4,3,2,1,0:T(8,128)} %get-tuple-element.8.own_rows, f32[64,256]{1,0:T(8,128)} %get-tuple-element.9.logits, s32[3,4,40,128]{3,2,1,0:T(8,128)} %get-tuple-element.10.own_tab, f32[1]{0:T(128)} %bitcast.4.lam_ref), custom_call_target="tpu_custom_call" | custom-call | tf_op jit(solution)/shard_map/exchange/pallas_call | solution.py:372
  63.4 1.5 %copy.11 = f32[64,256]{1,0:T(8,128)} copy(f32[64,256]{1,0:T(8,128)} %exchange.1) | data formatting | bytes 131072

commit v2 on v1

v2 whole, which is shorter than its diff:
```python
import functools

import jax
import jax.numpy as jnp
from jax import lax
from jax.experimental import pallas as pl
from jax.experimental.pallas import tpu as pltpu
from jax.sharding import PartitionSpec as P

F32, BF16, I32 = jnp.float32, jnp.bfloat16, jnp.int32
GROUPS = ((0, 16), (16, 8), (24, 8))
HALF = 32
LN, EN = 128, 1024
NT = (((1,), (1,)), ((), ()))


def iota(shape, axis):
    return lax.broadcasted_iota(I32, shape, axis)


def coordinates(n):
    device = lax.axis_index('model')
    return device, device % 2, (device // 2) % n, (device // (2 * n)) % n, device // (2 * n * n)


def local_kernel(n, tok_ref, bounds_ref, tau_ref, hid_hbm, w_hbm, keys_hbm, rows0, rows1, rows2, stat_out, logits_out, tab_out,
                 hid, w, keys, score, dedup, onehot, lohot, e3, in_sem, key_sem):
    inner = 2 * n * n
    _, _, cx, cy, cz = coordinates(n)
    in_copies = (pltpu.make_async_copy(hid_hbm, hid, in_sem.at[0]), pltpu.make_async_copy(w_hbm, w, in_sem.at[1]))
    for c in in_copies:
        c.start()
    kchunk = LN
    nk = keys.shape[0] // kchunk

    def key_copy(c):
        rows = pl.ds(c * kchunk, kchunk)
        return pltpu.make_async_copy(keys_hbm.at[rows], keys.at[rows], key_sem.at[c])

    for c in range(nk):
        key_copy(c).start()

    lane = iota((8, LN), 1)
    sub = iota((8, LN), 0)
    pos = sub * LN + lane

    def prev(a):
        r = pltpu.roll(a, 1, 1)
        return jnp.where(lane == 0, pltpu.roll(r, 1, 0), r)

    tok = tok_ref[...]
    first = ((tok != prev(tok)) | (pos == 0)).astype(I32)
    c = first
    for sh in (1, 2, 4, 8, 16, 32, 64):
        c = c + jnp.where(lane >= sh, pltpu.roll(c, sh, 1), 0)
    tot = jnp.broadcast_to(c[:, 127:LN], (8, LN))
    acc = tot
    for sh in (1, 2, 4):
        acc = acc + jnp.where(sub >= sh, pltpu.roll(acc, sh, 0), 0)
    rank = c + acc - tot - 1

    owner = tok // 256
    bnd = bounds_ref[...]
    nb = bnd.shape[1] - 1
    lo_b = jnp.broadcast_to(bnd[:, :nb], (8, nb))
    hi_b = jnp.broadcast_to(bnd[:, 1:], (8, nb))
    if nb < LN:
        lo_b = jnp.concatenate([lo_b, jnp.zeros((8, LN - nb), I32)], axis=1)
        hi_b = jnp.concatenate([hi_b, jnp.zeros((8, LN - nb), I32)], axis=1)
    counted = (pos >= jnp.take_along_axis(lo_b, owner, axis=1)) & (pos < jnp.take_along_axis(hi_b, owner, axis=1))
    rank_d = jnp.where(counted, rank, -1)
    for t in range(8):
        rows = iota((EN, LN), 0)
        dedup[:, t * LN:(t + 1) * LN] = jnp.where(rank_d[t:t + 1, :] == rows, 1.0, 0.0).astype(BF16)

    h = tok // LN
    tile_first = ((h != prev(h)) | (pos == 0)).astype(I32)
    half = h % 2
    jc = owner % 2
    jp = ((owner // 2) % n, (owner // (2 * n)) % n, owner // (2 * n * n))
    lo = tok % LN
    val = (first * (rank % LN + LN) * (1 + 255 * half)).astype(F32)
    starts = [(tile_first * jnp.where(half == hf, part, 0)).astype(F32)
              for hf in range(2) for part in (rank // LN, rank % LN)]
    sub32 = iota((32, LN), 0)
    for t in range(8):
        cols = slice(t * LN, (t + 1) * LN)
        r = slice(t, t + 1)
        lohot[0:LN, cols] = jnp.where(lo[r, :] == iota((LN, LN), 0), val[r, :], 0.0).astype(BF16)
        lohot[LN:160, cols] = jnp.where(
            sub32 < 8, starts[0][r, :], jnp.where(sub32 < 16, starts[1][r, :], jnp.where(
                sub32 < 24, starts[2][r, :], starts[3][r, :]))).astype(BF16)
    coord = (cx, cy, cz)
    for a, (b2, b3) in enumerate(((2, 1), (2, 0), (1, 0))):
        row = ((jp[a] - coord[a] + n) % n) * inner + jp[b2] * (2 * n) + jp[b3] * 2 + jc
        for t in range(8):
            onehot[:, t * LN:(t + 1) * LN] = jnp.where(
                row[t:t + 1, :] == iota((LN, LN), 0), 1.0, 0.0).astype(BF16)
        tb = lax.dot_general(onehot[...], lohot[0:LN, :], NT, preferred_element_type=F32).astype(I32)
        us = lax.dot_general(lohot[LN:160, :], onehot[...], NT, preferred_element_type=F32).astype(I32)
        for d in range(n):
            tab_out[a, d, 0:inner, :] = tb[d * inner:(d + 1) * inner, :]
            for hf in range(2):
                tab_out[a, d, inner + hf:inner + hf + 1, :] = us[16 * hf:16 * hf + 1] * LN + us[16 * hf + 8:16 * hf + 9]

    for c in in_copies:
        c.wait()
    lg = jnp.dot(hid[...], w[...], preferred_element_type=F32)
    logits_out[...] = lg
    lm = jnp.max(lg, axis=1, keepdims=True)
    lz = jnp.sum(jnp.exp(lg - lm), axis=1, keepdims=True)

    tau = tau_ref[0]

    def score_step(c, carry):
        key_copy(2 * c).wait()
        key_copy(2 * c + 1).wait()
        rows = pl.ds(c * 256, 256)
        cross = lax.dot_general(hid[...], keys[rows, :], NT, preferred_element_type=F32)
        sq = jnp.zeros((256, LN), F32)
        for t in range(keys.shape[1] // LN):
            k = keys[rows, t * LN:(t + 1) * LN].astype(F32)
            sq = sq + k * k
        norm = jnp.sum(sq.T, axis=0, keepdims=True)
        sc = (2.0 * cross - norm) / tau
        score[2 * c] = sc[:, :LN]
        score[2 * c + 1] = sc[:, LN:]
        return carry

    lax.fori_loop(0, nk // 2, score_step, 0)

    sc = [score[t] for t in range(8)]
    m = jnp.max(functools.reduce(jnp.maximum, sc), axis=1, keepdims=True)
    z = jnp.zeros((64, LN), F32)
    for t in range(8):
        e = jnp.exp(sc[t] - m)
        z = z + e
        hi = e.astype(BF16)
        r1 = e - hi.astype(F32)
        mid = r1.astype(BF16)
        low = (r1 - mid.astype(F32)).astype(BF16)
        cols = slice(t * LN, (t + 1) * LN)
        e3[0:64, cols] = hi
        e3[64:LN, cols] = mid
        e3[LN:192, cols] = low
    z = jnp.sum(z, axis=1, keepdims=True)
    l64 = iota((64, LN), 1)
    stat = jnp.where(l64 == 0, m, jnp.where(l64 == 1, z, jnp.where(l64 == 2, lm, lz)))
    row_outs = (rows0, rows1, rows2)
    for h in range(2):
        stat_out[h] = stat[h * HALF:(h + 1) * HALF]
        for out, (r0, nr) in zip(row_outs, GROUPS):
            out[h, 8] = stat[h * HALF + r0:h * HALF + r0 + nr]
    for c in range(4):
        dd = lax.dot_general(e3[...], dedup[c * 256:(c + 1) * 256, :], NT, preferred_element_type=F32)
        eu = dd[0:64] + (dd[64:LN] + dd[LN:192])
        for h in range(2):
            for out, (r0, nr) in zip(row_outs, GROUPS):
                for t in range(2):
                    out[h, 2 * c + t] = eu[h * HALF + r0:h * HALF + r0 + nr, t * LN:(t + 1) * LN]


def exchange_kernel(n, own0, own1, own2, own_stat, logits, own_tab, lam_ref, out_ref,
                    tab_pair, tab, tab_smem, list0, list1, list2, scaled0, scaled1, scaled2,
                    part20, part21, part22, relay0, relay1, relay2, recv20, recv21, recv22,
                    part30, part31, part32, recv30, recv31, recv32, fin, fin_in, stat_buf, stat_in,
                    swap_sem, tab_send, tab_recv, smem_sem, stat_send, stat_recv,
                    send1, recv1, send2, recv2_sem, send_relay, recv_relay, send3, recv3_sem):
    inner = 2 * n * n
    block = 4 * n
    device, core, cx, cy, cz = coordinates(n)
    other = 1 - core
    partner = device + 1 - 2 * core
    pcoord, pstride = (cx, cy, cz), (2, 2 * n, 2 * n * n)
    coord = (cx + core * (cy - cx), cy + core * (cx - cy), cz)
    stride = (2 + core * (2 * n - 2), 2 * n + core * (2 - 2 * n), 2 * n * n)
    axis_of = (core, other, 2)
    row_stride = ((2, 2 * n), (2 * n, 2), (2 + core * (2 * n - 2), 2 * n + core * (2 - 2 * n)))
    own, lists, scaled = (own0, own1, own2), (list0, list1, list2), (scaled0, scaled1, scaled2)
    part2, relay, recv2 = (part20, part21, part22), (relay0, relay1, relay2), (recv20, recv21, recv22)
    part3, recv3 = (part30, part31, part32), (recv30, recv31, recv32)

    def wrap(a):
        return lax.rem(a, n)

    def peer(v, d):
        return device + stride[v] * (wrap(coord[v] + d) - coord[v])

    def axis_peer(a, d):
        return device + pstride[a] * (wrap(pcoord[a] + d) - pcoord[a])

    def remote(src, dst, ssem, rsem, dev):
        return pltpu.make_async_remote_copy(src_ref=src, dst_ref=dst, send_sem=ssem, recv_sem=rsem,
                                            device_id={'model': dev}, device_id_type=pl.DeviceIdType.MESH)

    near = (1, n - 1) if n > 2 else (1,)
    far = tuple(range(2, n - 1))
    order = (1, 2, 0)
    sends = []

    def go(c):
        c.start()
        sends.append(c)

    barrier = pltpu.get_barrier_semaphore()
    partners = [partner] + [peer(v, d) for v in range(3) for d in range(1, n)]
    for p in partners:
        pl.semaphore_signal(barrier, inc=1, device_id={'model': p}, device_id_type=pl.DeviceIdType.MESH)
    for g in range(3):
        for i in range(2 * n):
            scaled[g][i, 8] = jnp.zeros(scaled[g].shape[2:], F32)
    pl.semaphore_wait(barrier, len(partners))

    stat_swap = remote(own_stat.at[other], stat_in.at[0], swap_sem.at[0, 0], swap_sem.at[1, 0], partner)
    tab_swap = remote(own_tab, tab_pair, swap_sem.at[0, 1], swap_sem.at[1, 1], partner)
    row_swap = [remote(own[g].at[other], lists[g].at[0], swap_sem.at[0, 2 + g], swap_sem.at[1, 2 + g], partner)
                for g in range(3)]
    go(stat_swap)
    go(tab_swap)
    for g in order:
        go(row_swap[g])

    def tab_copy(a, d, l):
        src = own_tab if l == 0 else tab_pair
        return remote(src.at[a, d], tab.at[a, n - d - 1, l], tab_send.at[a, d - 1, l], tab_recv.at[a, n - d - 1, l],
                      axis_peer(a, d))

    def row_copy(g, d, l):
        src = own[g].at[core] if l == 0 else lists[g].at[0]
        return remote(src, lists[g].at[2 * (n - d) - 1 + l], send1.at[g, d - 1, l], recv1.at[g, n - d - 1, l], peer(g, d))

    def row_relay(g, l):
        frm, to = (n - 1, 1) if l == 0 else (1, n - 1)
        return remote(lists[g].at[2 * frm - 1 + l], lists[g].at[3 + l], send1.at[g, 1, l], recv1.at[g, 1, l], peer(g, to))

    for d in far + near:
        for a in range(3):
            go(tab_copy(a, d, 0))
    for d in near:
        for g in order:
            go(row_copy(g, d, 0))

    def combine(tiles):
        ln = iota((HALF, LN), 1)
        ms = [jnp.broadcast_to(t[:, 0:1], (HALF, LN)) for t in tiles]
        ls = [jnp.broadcast_to(t[:, 2:3], (HALF, LN)) for t in tiles]
        mm = functools.reduce(jnp.maximum, ms)
        ll = functools.reduce(jnp.maximum, ls)
        zz = sum(jnp.exp(a - mm) * t[:, 1:2] for a, t in zip(ms, tiles))
        lzz = sum(jnp.exp(a - ll) * t[:, 3:4] for a, t in zip(ls, tiles))
        return jnp.where(ln == 0, mm, jnp.where(ln == 1, zz, jnp.where(ln == 2, ll, lzz)))

    def stat_copy(v, d):
        return remote(stat_buf.at[v], stat_in.at[1 + v * (n - 1) + n - d - 1], stat_send.at[v, d - 1],
                      stat_recv.at[v, n - d - 1], peer(v, d))

    def stat_round(v):
        for d in range(1, n):
            stat_copy(v, d).wait_recv()
        stat_buf[v + 1] = combine([stat_buf[v]] + [stat_in[1 + v * (n - 1) + k] for k in range(n - 1)])
        if v < 2:
            for d in range(1, n):
                go(stat_copy(v + 1, d))

    stat_swap.wait_recv()
    stat_buf[0] = combine([own_stat[core], stat_in[0]])
    for d in range(1, n):
        go(stat_copy(0, d))
    tab_swap.wait_recv()
    for d in far + near:
        for a in range(3):
            go(tab_copy(a, d, 1))
    for g in order:
        row_swap[g].wait_recv()
        for d in near:
            go(row_copy(g, d, 1))
    stat_round(0)
    for g in order:
        for d in near:
            for l in range(2):
                row_copy(g, d, l).wait_recv()
        if far:
            for l in range(2):
                go(row_relay(g, l))
    stat_round(1)

    def tab_of(a, k, l):
        if k:
            return tab.at[a, k - 1, l]
        return (tab_pair if l else own_tab).at[a, 0]

    def list_of(g, k, l):
        if k == 0 and l == 0:
            return own[g].at[core]
        return lists[g].at[2 * k - 1 + l]

    for d in range(1, n):
        for l in range(2):
            for a in range(3):
                tab_copy(a, d, l).wait_recv()
    smem_copies = [pltpu.make_async_copy(tab_of(a, k, l).at[pl.ds(inner, 2)], tab_smem.at[a, k, l], smem_sem.at[a, k, l])
                   for a in range(3) for k in range(n) for l in range(2)]
    for c in smem_copies:
        c.start()
    stat_round(2)
    stat_back = remote(stat_buf.at[3], stat_in.at[3 * n - 2], swap_sem.at[0, 5], swap_sem.at[1, 5], partner)
    go(stat_back)
    for c in smem_copies:
        c.wait()

    src = [(k, l) for k in range(n) for l in range(2)]
    for g in order:
        if far:
            for l in range(2):
                row_relay(g, l).wait_recv()

    def scale(g):
        r0, nr = GROUPS[g]
        mm = stat_buf[3, r0:r0 + nr, 0:1]
        for i, (k, l) in enumerate(src):
            rows = list_of(g, k, l)
            f = jnp.broadcast_to(jnp.exp(rows[8][:, 0:1] - mm), (nr, LN))
            for t in range(8):
                scaled[g][i, t] = rows[t] * f

    def partial_hist(g, d2):
        nr = GROUPS[g][1]
        a = axis_of[g]
        c2, c3 = coord[(g + 1) % 3], coord[(g + 2) % 3]
        s2, s3 = row_stride[g]
        base = wrap(c2 + d2) * s2
        ln = iota((nr, LN), 1)

        def pair_step(q, carry):
            d3 = lax.div(q, 2)
            c = q - 2 * d3
            row = base + wrap(c3 + d3) * s3 + c
            acc = [jnp.zeros((nr, LN), F32)] * 2
            for i, (k, l) in enumerate(src):
                packed = jnp.broadcast_to(tab_of(a, k, l)[pl.ds(row, 1), :], (nr, LN))
                for hf in range(2):
                    u = tab_smem[a, k, l, hf, ((n - k) % n) * inner + row]
                    kt = lax.shift_right_logical(u, 7)
                    merged = jnp.where(ln >= (u & 127), scaled[g][i, kt], scaled[g][i, kt + 1])
                    code = lax.shift_right_logical(packed, 8) if hf else packed
                    got = jnp.take_along_axis(merged, code & 127, axis=1)
                    acc[hf] = acc[hf] + jnp.where((code & LN) != 0, got, 0.0)
            part2[g][d2, 2 * q] = acc[0]
            part2[g][d2, 2 * q + 1] = acc[1]
            return carry

        lax.fori_loop(0, 2 * n, pair_step, 0, unroll=2)

    def copy2(g, d):
        i = 0 if d == 1 else 1
        return remote(part2[g].at[d], recv2[g].at[i], send2.at[g, i], recv2_sem.at[g, i], peer((g + 1) % 3, d))

    halves = (pl.ds(0, block // 2), pl.ds(block // 2, block // 2))

    def copy2_relay(g, i):
        return remote(part2[g].at[2, halves[i]], relay[g].at[i], send_relay.at[g, i], recv_relay.at[g, i],
                      peer((g + 1) % 3, near[i]))

    def copy3(g, d):
        return remote(part3[g].at[d], recv3[g].at[n - d - 1], send3.at[g, d - 1], recv3_sem.at[g, n - d - 1],
                      peer((g + 2) % 3, d))

    for g in order:
        scale(g)
        for d2 in far:
            partial_hist(g, d2)
            for i in range(2):
                go(copy2_relay(g, i))
    for g in order:
        for d2 in near:
            partial_hist(g, d2)
    for g in order:
        for i, d2 in enumerate(near):
            if far:
                copy2_relay(g, i).wait_recv()
                for t in range(block // 2):
                    q = i * (block // 2) + t
                    part2[g][d2, q] = part2[g][d2, q] + relay[g][i, t]
            go(copy2(g, d2))
    for g in order:
        partial_hist(g, 0)

    for g in order:
        for d in near:
            copy2(g, d).wait_recv()
        for d3 in far + near + (0,):
            for ch in range(4):
                q = d3 * 4 + ch
                part3[g][d3, ch] = part2[g][0, q] + sum(recv2[g][i, q] for i in range(len(near)))
            if d3:
                go(copy3(g, d3))

    for g in order:
        r0, nr = GROUPS[g]
        for d in range(1, n):
            copy3(g, d).wait_recv()
        for ch in range(4):
            fin[ch // 2, ch % 2, r0:r0 + nr] = part3[g][0, ch] + sum(recv3[g][k, ch] for k in range(n - 1))

    back = remote(fin.at[other], fin_in, swap_sem.at[0, 6], swap_sem.at[1, 6], partner)
    go(back)
    lam = lam_ref[0]

    def finish(block_ref, st, rows_half):
        zz, ll, lzz = st[:, 1:2], st[:, 2:3], st[:, 3:4]
        rows = pl.ds(pl.multiple_of(rows_half * HALF, 8), HALF)
        for hf in range(2):
            cols = slice(hf * LN, (hf + 1) * LN)
            lm_exp = jnp.exp(logits[rows, cols] - ll)
            out_ref[rows, cols] = jnp.log(lam * (block_ref[hf] / zz) + (1.0 - lam) * (lm_exp / lzz))

    finish(fin.at[core], stat_buf[3], core)
    stat_back.wait_recv()
    back.wait_recv()
    finish(fin_in, stat_in[3 * n - 2], other)
    for c in sends:
        c.wait_send()


def step(n, hidden, w_local, keys_local, tok_local, bounds_local, tau, lam):
    tab_rows = 2 * n * n + 8
    block = 4 * n
    dim = hidden.shape[1]
    V, DMA = pltpu.VMEM, pltpu.SemaphoreType.DMA
    vm = pl.BlockSpec(memory_space=pltpu.VMEM)
    sm = pl.BlockSpec(memory_space=pltpu.SMEM)
    hbm = pl.BlockSpec(memory_space=pl.ANY)
    *rows, stat, logits, tab = pl.pallas_call(
        functools.partial(local_kernel, n),
        out_shape=tuple(jax.ShapeDtypeStruct((2, 9, nr, LN), F32) for _, nr in GROUPS) + (
            jax.ShapeDtypeStruct((2, HALF, LN), F32), jax.ShapeDtypeStruct((64, 256), F32),
            jax.ShapeDtypeStruct((3, n, tab_rows, LN), I32)),
        in_specs=[vm, vm, sm, hbm, hbm, hbm],
        out_specs=(vm,) * 6,
        scratch_shapes=[
            V((64, dim), BF16), V((dim, 256), BF16), V((EN, dim), BF16), V((8, 64, LN), F32),
            V((EN, EN), BF16), V((LN, EN), BF16), V((160, EN), BF16), V((192, EN), BF16),
            DMA((2,)), DMA((8,))],
        name='local_scores',
    )(tok_local.reshape(8, LN), bounds_local, tau.reshape(1), hidden, w_local, keys_local)

    def per_group(*lead):
        return [V((*lead, nr, LN), F32) for _, nr in GROUPS]

    m = n - 1
    return pl.pallas_call(
        functools.partial(exchange_kernel, n),
        out_shape=jax.ShapeDtypeStruct((64, 256), F32),
        in_specs=[vm] * 6 + [sm],
        out_specs=vm,
        scratch_shapes=[
            V((3, n, tab_rows, LN), I32), V((3, m, 2, tab_rows, LN), I32), pltpu.SMEM((3, n, 2, 2, LN), I32),
            *per_group(2 * n - 1, 9), *per_group(2 * n, 9), *per_group(n, block), *per_group(2, block // 2),
            *per_group(2, block), *per_group(n, 4), *per_group(m, 4),
            V((2, 2, HALF, LN), F32), V((2, HALF, LN), F32), V((4, HALF, LN), F32), V((3 * n - 1, HALF, LN), F32),
            DMA((2, 7)), DMA((3, m, 2)), DMA((3, m, 2)), DMA((3, n, 2)), DMA((3, m)), DMA((3, m)),
            DMA((3, m, 2)), DMA((3, m, 2)), DMA((3, 2)), DMA((3, 2)), DMA((3, 2)), DMA((3, 2)), DMA((3, m)), DMA((3, m))],
        compiler_params=pltpu.CompilerParams(collective_id=0, has_side_effects=True),
        name='exchange',
    )(*rows, stat, logits, tab, lam.reshape(1))


def solution(mesh):
    n = round((mesh.shape['model'] // 2) ** (1 / 3))
    return jax.shard_map(functools.partial(step, n), mesh=mesh,
                         in_specs=(P('data', None), P(None, 'model'), P('model', None), P('model'),
                                   P('model', None), P(), P()),
                         out_specs=P('data', 'model'), check_vma=False)
```

time: 65.1 us -> 56.1 us (0.86)
  Pallas kernels: 62 us -> 53.1 us
    pallas_call x1, Pallas kernels: 50.4 us -> 41.5 us  [step(): pl.pallas_call(functools.partial(exchange_kernel, n), out_shape=jax.Shape...]
where the time goes in v2:
time: 56.1 us; the launch traced here: 55.9 us
  Pallas kernels  53.1 us (95%)
  local copies, waits for them, and re-layouts  1.47 us (3%)
  between operations  1.31 us (2%)
    pallas_call x1, Pallas kernels, step(): pl.pallas_call(functools.partial(exchange_kernel, n), out_shape=jax.Shape...  41.5 us
    pallas_call x1, Pallas kernels, step(): pl.pallas_call(functools.partial(local_kernel, n), out_shape=tuple((jax.S...  11.7 us
    unnamed x1, local copies, waits for them, and re-layouts  1.47 us

profile of v2, /device:TPU:1, one launch (start us, length us, event | category | flops | bytes accessed | tf_op | source)
XLA Modules:
  0.0 55.9 jit_solution(1203110271930283067)
XLA Ops:
  1.3 11.7 %local_scores.1 = (f32[2,9,16,128]{3,2,1,0:T(8,128)}, f32[2,9,8,128]{3,2,1,0:T(8,128)}, f32[2,9,8,128]{3,2,1,0:T(8,128)}, f32[2,32,128]{2,1,0:T(8,128)}, f32[64,256]{1,0:T(8,128)}, /*index=5*/s32[3,4,40,128]{3,2,1,0:T(8,128)}) custom-call(s32[8,128]{1,0:T(8,128)} %bitcast.5, s32[1,129]{1,0:T(1,128)} %bounds_ref.1, f32[1]{0:T(128)} %bitcast.3.tau_ref, ...), custom_call_target="tpu_custom_call" | custom-call | tf_op jit(solution)/shard_map/local_scores/pallas_call | solution.py:433
  13.0 41.5 %exchange.1 = f32[64,256]{1,0:T(8,128)} custom-call(f32[2,9,16,128]{3,2,1,0:T(8,128)} %get-tuple-element.11.own0, f32[2,9,8,128]{3,2,1,0:T(8,128)} %get-tuple-element.12.own1, f32[2,9,8,128]{3,2,1,0:T(8,128)} %get-tuple-element.13.own2, f32[2,32,128]{2,1,0:T(8,128)} %get-tuple-element.14.own_stat, f32[64,256]{1,0:T(8,128)} %get-tuple-element.15.logits, ...), custom_call_target="tpu_custom_call" | custom-call | tf_op jit(solution)/shard_map/exchange/pallas_call | solution.py:451
  54.5 1.5 %copy.11 = f32[64,256]{1,0:T(8,128)} copy(f32[64,256]{1,0:T(8,128)} %exchange.1) | data formatting | bytes 131072

commit v3 on v2

--- a/solution.py
+++ b/solution.py
@@ -9,6 +9,7 @@
 
 F32, BF16, I32 = jnp.float32, jnp.bfloat16, jnp.int32
 GROUPS = ((0, 16), (16, 8), (24, 8))
+UNROLL = 2
 HALF = 32
 LN, EN = 128, 1024
 NT = (((1,), (1,)), ((), ()))
@@ -23,7 +24,7 @@
     return device, device % 2, (device // 2) % n, (device // (2 * n)) % n, device // (2 * n * n)
 
 
-def local_kernel(n, tok_ref, bounds_ref, tau_ref, hid_hbm, w_hbm, keys_hbm, rows0, rows1, rows2, stat_out, logits_out, tab_out,
+def local_kernel(n, tok_ref, bounds_ref, tau_ref, hid_hbm, w_hbm, keys_hbm, rows0, rows1, rows2, logits_out, tab_out,
                  hid, w, keys, score, dedup, onehot, lohot, e3, in_sem, key_sem):
     inner = 2 * n * n
     _, _, cx, cy, cz = coordinates(n)
@@ -148,7 +149,6 @@
     stat = jnp.where(l64 == 0, m, jnp.where(l64 == 1, z, jnp.where(l64 == 2, lm, lz)))
     row_outs = (rows0, rows1, rows2)
     for h in range(2):
-        stat_out[h] = stat[h * HALF:(h + 1) * HALF]
         for out, (r0, nr) in zip(row_outs, GROUPS):
             out[h, 8] = stat[h * HALF + r0:h * HALF + r0 + nr]
     for c in range(4):
@@ -160,22 +160,27 @@
                     out[h, 2 * c + t] = eu[h * HALF + r0:h * HALF + r0 + nr, t * LN:(t + 1) * LN]
 
 
-def exchange_kernel(n, own0, own1, own2, own_stat, logits, own_tab, lam_ref, out_ref,
+def exchange_kernel(n, own0, own1, own2, logits, own_tab, lam_ref, out_ref,
                     tab_pair, tab, tab_smem, list0, list1, list2, scaled0, scaled1, scaled2,
                     part20, part21, part22, relay0, relay1, relay2, recv20, recv21, recv22,
-                    part30, part31, part32, recv30, recv31, recv32, fin, fin_in, stat_buf, stat_in,
-                    swap_sem, tab_send, tab_recv, smem_sem, stat_send, stat_recv,
+                    part30, part31, part32, recv30, recv31, recv32, fin, fin_in,
+                    swap_sem, tab_send, tab_recv, smem_sem,
                     send1, recv1, send2, recv2_sem, send_relay, recv_relay, send3, recv3_sem):
     inner = 2 * n * n
-    block = 4 * n
+    mid = 2 * n
+    block = 2 * mid
     device, core, cx, cy, cz = coordinates(n)
     other = 1 - core
     partner = device + 1 - 2 * core
     pcoord, pstride = (cx, cy, cz), (2, 2 * n, 2 * n * n)
-    coord = (cx + core * (cy - cx), cy + core * (cx - cy), cz)
-    stride = (2 + core * (2 * n - 2), 2 * n + core * (2 - 2 * n), 2 * n * n)
+
+    def axes_of(c):
+        return ((cx + c * (cy - cx), cy + c * (cx - cy), cz), (2 + c * (2 * n - 2), 2 * n + c * (2 - 2 * n), 2 * n * n))
+
+    coord, stride = axes_of(core)
+    coord_o, stride_o = axes_of(other)
     axis_of = (core, other, 2)
-    row_stride = ((2, 2 * n), (2 * n, 2), (2 + core * (2 * n - 2), 2 * n + core * (2 - 2 * n)))
+    row_stride = ((2, 2 * n), (2 * n, 2), (stride[0], stride[1]))
     own, lists, scaled = (own0, own1, own2), (list0, list1, list2), (scaled0, scaled1, scaled2)
     part2, relay, recv2 = (part20, part21, part22), (relay0, relay1, relay2), (recv20, recv21, recv22)
     part3, recv3 = (part30, part31, part32), (recv30, recv31, recv32)
@@ -186,8 +191,11 @@
     def peer(v, d):
         return device + stride[v] * (wrap(coord[v] + d) - coord[v])
 
-    def axis_peer(a, d):
-        return device + pstride[a] * (wrap(pcoord[a] + d) - pcoord[a])
+    def peer_other(v, d):
+        return partner + stride_o[v] * (wrap(coord_o[v] + d) - coord_o[v])
+
+    def axis_peer(start, a, d):
+        return start + pstride[a] * (wrap(pcoord[a] + d) - pcoord[a])
 
     def remote(src, dst, ssem, rsem, dev):
         return pltpu.make_async_remote_copy(src_ref=src, dst_ref=dst, send_sem=ssem, recv_sem=rsem,
@@ -203,7 +211,7 @@
         sends.append(c)
 
     barrier = pltpu.get_barrier_semaphore()
-    partners = [partner] + [peer(v, d) for v in range(3) for d in range(1, n)]
+    partners = [partner] + [axis_peer(start, a, d) for start in (device, partner) for a in range(3) for d in range(1, n)]
     for p in partners:
         pl.semaphore_signal(barrier, inc=1, device_id={'model': p}, device_id_type=pl.DeviceIdType.MESH)
     for g in range(3):
@@ -211,70 +219,47 @@
             scaled[g][i, 8] = jnp.zeros(scaled[g].shape[2:], F32)
     pl.semaphore_wait(barrier, len(partners))
 
-    stat_swap = remote(own_stat.at[other], stat_in.at[0], swap_sem.at[0, 0], swap_sem.at[1, 0], partner)
-    tab_swap = remote(own_tab, tab_pair, swap_sem.at[0, 1], swap_sem.at[1, 1], partner)
-    row_swap = [remote(own[g].at[other], lists[g].at[0], swap_sem.at[0, 2 + g], swap_sem.at[1, 2 + g], partner)
+    tab_swap = remote(own_tab.at[:, 0], tab_pair, swap_sem.at[0, 0], swap_sem.at[1, 0], partner)
+    row_swap = [remote(own[g].at[other], lists[g].at[0], swap_sem.at[0, 1 + g], swap_sem.at[1, 1 + g], partner)
                 for g in range(3)]
-    go(stat_swap)
-    go(tab_swap)
-    for g in order:
-        go(row_swap[g])
 
     def tab_copy(a, d, l):
-        src = own_tab if l == 0 else tab_pair
-        return remote(src.at[a, d], tab.at[a, n - d - 1, l], tab_send.at[a, d - 1, l], tab_recv.at[a, n - d - 1, l],
-                      axis_peer(a, d))
+        return remote(own_tab.at[a, d], tab.at[a, n - d - 1, l], tab_send.at[a, d - 1, l], tab_recv.at[a, n - d - 1, l],
+                      axis_peer(partner if l else device, a, d))
 
     def row_copy(g, d, l):
-        src = own[g].at[core] if l == 0 else lists[g].at[0]
-        return remote(src, lists[g].at[2 * (n - d) - 1 + l], send1.at[g, d - 1, l], recv1.at[g, n - d - 1, l], peer(g, d))
+        return remote(own[g].at[other if l else core], lists[g].at[2 * (n - d) - 1 + l], send1.at[g, d - 1, l],
+                      recv1.at[g, n - d - 1, l], peer_other(g, d) if l else peer(g, d))
 
     def row_relay(g, l):
         frm, to = (n - 1, 1) if l == 0 else (1, n - 1)
         return remote(lists[g].at[2 * frm - 1 + l], lists[g].at[3 + l], send1.at[g, 1, l], recv1.at[g, 1, l], peer(g, to))
 
+    for g in order:
+        for d in near:
+            for l in range(2):
+                go(row_copy(g, d, l))
+    for g in order:
+        go(row_swap[g])
+    go(tab_swap)
     for d in far + near:
         for a in range(3):
-            go(tab_copy(a, d, 0))
-    for d in near:
-        for g in order:
-            go(row_copy(g, d, 0))
-
-    def combine(tiles):
-        ln = iota((HALF, LN), 1)
-        ms = [jnp.broadcast_to(t[:, 0:1], (HALF, LN)) for t in tiles]
-        ls = [jnp.broadcast_to(t[:, 2:3], (HALF, LN)) for t in tiles]
+            for l in range(2):
+                go(tab_copy(a, d, l))
+
+    def stats(tiles, counted=None):
+        shape = tiles[0].shape
+        ln = iota(shape, 1)
+        counted = counted or tiles
+        ms = [jnp.broadcast_to(t[:, 0:1], shape) for t in tiles]
+        ls = [jnp.broadcast_to(t[:, 2:3], shape) for t in tiles]
         mm = functools.reduce(jnp.maximum, ms)
         ll = functools.reduce(jnp.maximum, ls)
-        zz = sum(jnp.exp(a - mm) * t[:, 1:2] for a, t in zip(ms, tiles))
-        lzz = sum(jnp.exp(a - ll) * t[:, 3:4] for a, t in zip(ls, tiles))
-        return jnp.where(ln == 0, mm, jnp.where(ln == 1, zz, jnp.where(ln == 2, ll, lzz)))
-
-    def stat_copy(v, d):
-        return remote(stat_buf.at[v], stat_in.at[1 + v * (n - 1) + n - d - 1], stat_send.at[v, d - 1],
-                      stat_recv.at[v, n - d - 1], peer(v, d))
-
-    def stat_round(v):
-        for d in range(1, n):
-            stat_copy(v, d).wait_recv()
-        stat_buf[v + 1] = combine([stat_buf[v]] + [stat_in[1 + v * (n - 1) + k] for k in range(n - 1)])
-        if v < 2:
-            for d in range(1, n):
-                go(stat_copy(v + 1, d))
-
-    stat_swap.wait_recv()
-    stat_buf[0] = combine([own_stat[core], stat_in[0]])
-    for d in range(1, n):
-        go(stat_copy(0, d))
-    tab_swap.wait_recv()
-    for d in far + near:
-        for a in range(3):
-            go(tab_copy(a, d, 1))
-    for g in order:
-        row_swap[g].wait_recv()
-        for d in near:
-            go(row_copy(g, d, 1))
-    stat_round(0)
+        fs = [jnp.exp(a - mm) for a in ms]
+        zz = sum(f * t[:, 1:2] for f, t in zip(fs, counted))
+        lzz = sum(jnp.exp(a - ll) * t[:, 3:4] for a, t in zip(ls, counted))
+        return fs, jnp.where(ln == 0, mm, jnp.where(ln == 1, zz, jnp.where(ln == 2, ll, lzz)))
+
     for g in order:
         for d in near:
             for l in range(2):
@@ -282,46 +267,32 @@
         if far:
             for l in range(2):
                 go(row_relay(g, l))
-    stat_round(1)
+        row_swap[g].wait_recv()
 
     def tab_of(a, k, l):
         if k:
             return tab.at[a, k - 1, l]
-        return (tab_pair if l else own_tab).at[a, 0]
+        return tab_pair.at[a] if l else own_tab.at[a, 0]
 
     def list_of(g, k, l):
         if k == 0 and l == 0:
             return own[g].at[core]
         return lists[g].at[2 * k - 1 + l]
 
+    tab_swap.wait_recv()
     for d in range(1, n):
         for l in range(2):
             for a in range(3):
                 tab_copy(a, d, l).wait_recv()
-    smem_copies = [pltpu.make_async_copy(tab_of(a, k, l).at[pl.ds(inner, 2)], tab_smem.at[a, k, l], smem_sem.at[a, k, l])
-                   for a in range(3) for k in range(n) for l in range(2)]
+    smem_copies = [pltpu.make_async_copy(tab_of(axis_of[g], k, l).at[pl.ds(inner, 2)], tab_smem.at[g, k, l],
+                                         smem_sem.at[g, k, l])
+                   for g in range(3) for k in range(n) for l in range(2)]
     for c in smem_copies:
         c.start()
-    stat_round(2)
-    stat_back = remote(stat_buf.at[3], stat_in.at[3 * n - 2], swap_sem.at[0, 5], swap_sem.at[1, 5], partner)
-    go(stat_back)
     for c in smem_copies:
         c.wait()
 
     src = [(k, l) for k in range(n) for l in range(2)]
-    for g in order:
-        if far:
-            for l in range(2):
-                row_relay(g, l).wait_recv()
-
-    def scale(g):
-        r0, nr = GROUPS[g]
-        mm = stat_buf[3, r0:r0 + nr, 0:1]
-        for i, (k, l) in enumerate(src):
-            rows = list_of(g, k, l)
-            f = jnp.broadcast_to(jnp.exp(rows[8][:, 0:1] - mm), (nr, LN))
-            for t in range(8):
-                scaled[g][i, t] = rows[t] * f
 
     def partial_hist(g, d2):
         nr = GROUPS[g][1]
@@ -339,24 +310,25 @@
             for i, (k, l) in enumerate(src):
                 packed = jnp.broadcast_to(tab_of(a, k, l)[pl.ds(row, 1), :], (nr, LN))
                 for hf in range(2):
-                    u = tab_smem[a, k, l, hf, ((n - k) % n) * inner + row]
+                    u = tab_smem[g, k, l, hf, ((n - k) % n) * inner + row]
                     kt = lax.shift_right_logical(u, 7)
                     merged = jnp.where(ln >= (u & 127), scaled[g][i, kt], scaled[g][i, kt + 1])
                     code = lax.shift_right_logical(packed, 8) if hf else packed
-                    got = jnp.take_along_axis(merged, code & 127, axis=1)
+                    got = jnp.take_along_axis(merged, code & 127, axis=1, mode='promise_in_bounds')
                     acc[hf] = acc[hf] + jnp.where((code & LN) != 0, got, 0.0)
-            part2[g][d2, 2 * q] = acc[0]
-            part2[g][d2, 2 * q + 1] = acc[1]
+            t = 2 * q + lax.div(q, n)
+            part2[g][d2, t] = acc[0]
+            part2[g][d2, t + 1] = acc[1]
             return carry
 
-        lax.fori_loop(0, 2 * n, pair_step, 0, unroll=2)
+        lax.fori_loop(0, mid, pair_step, 0, unroll=UNROLL)
+
+    halves = (pl.ds(0, mid + 1), pl.ds(mid, mid + 1))
 
     def copy2(g, d):
         i = 0 if d == 1 else 1
         return remote(part2[g].at[d], recv2[g].at[i], send2.at[g, i], recv2_sem.at[g, i], peer((g + 1) % 3, d))
 
-    halves = (pl.ds(0, block // 2), pl.ds(block // 2, block // 2))
-
     def copy2_relay(g, i):
         return remote(part2[g].at[2, halves[i]], relay[g].at[i], send_relay.at[g, i], recv_relay.at[g, i],
                       peer((g + 1) % 3, near[i]))
@@ -365,8 +337,18 @@
         return remote(part3[g].at[d], recv3[g].at[n - d - 1], send3.at[g, d - 1], recv3_sem.at[g, n - d - 1],
                       peer((g + 2) % 3, d))
 
-    for g in order:
-        scale(g)
+    group_stat = {}
+    for g in order:
+        if far:
+            for l in range(2):
+                row_relay(g, l).wait_recv()
+        fs, group_stat[g] = stats([list_of(g, k, l)[8] for k, l in src])
+        for i, (k, l) in enumerate(src):
+            rows = list_of(g, k, l)
+            for t in range(8):
+                scaled[g][i, t] = rows[t] * fs[i]
+        for d2 in far + near + (0,):
+            part2[g][d2, mid] = group_stat[g]
         for d2 in far:
             partial_hist(g, d2)
             for i in range(2):
@@ -378,9 +360,17 @@
         for i, d2 in enumerate(near):
             if far:
                 copy2_relay(g, i).wait_recv()
-                for t in range(block // 2):
-                    q = i * (block // 2) + t
-                    part2[g][d2, q] = part2[g][d2, q] + relay[g][i, t]
+                there = relay[g][i, 0 if i else mid]
+                zero = jnp.zeros(there.shape, F32)
+                fs, tile = stats([group_stat[g], there], [group_stat[g], zero if i else there])
+                for t in range(block + 1):
+                    r = t - i * mid
+                    if t == mid:
+                        part2[g][d2, t] = tile
+                    elif 0 <= r <= mid:
+                        part2[g][d2, t] = part2[g][d2, t] * fs[0] + relay[g][i, r] * fs[1]
+                    else:
+                        part2[g][d2, t] = part2[g][d2, t] * fs[0]
             go(copy2(g, d2))
     for g in order:
         partial_hist(g, 0)
@@ -388,10 +378,14 @@
     for g in order:
         for d in near:
             copy2(g, d).wait_recv()
+        parts = [part2[g].at[0]] + [recv2[g].at[i] for i in range(len(near))]
+        fs, tile = stats([p[mid] for p in parts])
         for d3 in far + near + (0,):
             for ch in range(4):
                 q = d3 * 4 + ch
-                part3[g][d3, ch] = part2[g][0, q] + sum(recv2[g][i, q] for i in range(len(near)))
+                q = q + q // mid
+                part3[g][d3, ch] = sum(p[q] * f for p, f in zip(parts, fs))
+            part3[g][d3, 4] = tile
             if d3:
                 go(copy3(g, d3))
 
@@ -399,14 +393,19 @@
         r0, nr = GROUPS[g]
         for d in range(1, n):
             copy3(g, d).wait_recv()
+        parts = [part3[g].at[0]] + [recv3[g].at[k] for k in range(n - 1)]
+        fs, tile = stats([p[4] for p in parts])
         for ch in range(4):
-            fin[ch // 2, ch % 2, r0:r0 + nr] = part3[g][0, ch] + sum(recv3[g][k, ch] for k in range(n - 1))
-
-    back = remote(fin.at[other], fin_in, swap_sem.at[0, 6], swap_sem.at[1, 6], partner)
+            fin[ch // 2, ch % 2, r0:r0 + nr] = sum(p[ch] * f for p, f in zip(parts, fs))
+        for c in range(2):
+            fin[c, 2, r0:r0 + nr] = tile
+
+    back = remote(fin.at[other], fin_in, swap_sem.at[0, 4], swap_sem.at[1, 4], partner)
     go(back)
     lam = lam_ref[0]
 
-    def finish(block_ref, st, rows_half):
+    def finish(block_ref, rows_half):
+        st = block_ref[2]
         zz, ll, lzz = st[:, 1:2], st[:, 2:3], st[:, 3:4]
         rows = pl.ds(pl.multiple_of(rows_half * HALF, 8), HALF)
         for hf in range(2):
@@ -414,10 +413,9 @@
             lm_exp = jnp.exp(logits[rows, cols] - ll)
             out_ref[rows, cols] = jnp.log(lam * (block_ref[hf] / zz) + (1.0 - lam) * (lm_exp / lzz))
 
-    finish(fin.at[core], stat_buf[3], core)
-    stat_back.wait_recv()
+    finish(fin.at[core], core)
     back.wait_recv()
-    finish(fin_in, stat_in[3 * n - 2], other)
+    finish(fin_in, other)
     for c in sends:
         c.wait_send()
 
@@ -430,13 +428,13 @@
     vm = pl.BlockSpec(memory_space=pltpu.VMEM)
     sm = pl.BlockSpec(memory_space=pltpu.SMEM)
     hbm = pl.BlockSpec(memory_space=pl.ANY)
-    *rows, stat, logits, tab = pl.pallas_call(
+    *rows, logits, tab = pl.pallas_call(
         functools.partial(local_kernel, n),
         out_shape=tuple(jax.ShapeDtypeStruct((2, 9, nr, LN), F32) for _, nr in GROUPS) + (
-            jax.ShapeDtypeStruct((2, HALF, LN), F32), jax.ShapeDtypeStruct((64, 256), F32),
+            jax.ShapeDtypeStruct((64, 256), F32),
             jax.ShapeDtypeStruct((3, n, tab_rows, LN), I32)),
         in_specs=[vm, vm, sm, hbm, hbm, hbm],
-        out_specs=(vm,) * 6,
+        out_specs=(vm,) * 5,
         scratch_shapes=[
             V((64, dim), BF16), V((dim, 256), BF16), V((EN, dim), BF16), V((8, 64, LN), F32),
             V((EN, EN), BF16), V((LN, EN), BF16), V((160, EN), BF16), V((192, EN), BF16),
@@ -451,18 +449,18 @@
     return pl.pallas_call(
         functools.partial(exchange_kernel, n),
         out_shape=jax.ShapeDtypeStruct((64, 256), F32),
-        in_specs=[vm] * 6 + [sm],
+        in_specs=[vm] * 5 + [sm],
         out_specs=vm,
         scratch_shapes=[
-            V((3, n, tab_rows, LN), I32), V((3, m, 2, tab_rows, LN), I32), pltpu.SMEM((3, n, 2, 2, LN), I32),
-            *per_group(2 * n - 1, 9), *per_group(2 * n, 9), *per_group(n, block), *per_group(2, block // 2),
-            *per_group(2, block), *per_group(n, 4), *per_group(m, 4),
-            V((2, 2, HALF, LN), F32), V((2, HALF, LN), F32), V((4, HALF, LN), F32), V((3 * n - 1, HALF, LN), F32),
-            DMA((2, 7)), DMA((3, m, 2)), DMA((3, m, 2)), DMA((3, n, 2)), DMA((3, m)), DMA((3, m)),
+            V((3, tab_rows, LN), I32), V((3, m, 2, tab_rows, LN), I32), pltpu.SMEM((3, n, 2, 2, LN), I32),
+            *per_group(2 * n - 1, 9), *per_group(2 * n, 9), *per_group(n, block + 1), *per_group(2, block // 2 + 1),
+            *per_group(2, block + 1), *per_group(n, 5), *per_group(m, 5),
+            V((2, 3, HALF, LN), F32), V((3, HALF, LN), F32),
+            DMA((2, 5)), DMA((3, m, 2)), DMA((3, m, 2)), DMA((3, n, 2)),
             DMA((3, m, 2)), DMA((3, m, 2)), DMA((3, 2)), DMA((3, 2)), DMA((3, 2)), DMA((3, 2)), DMA((3, m)), DMA((3, m))],
         compiler_params=pltpu.CompilerParams(collective_id=0, has_side_effects=True),
         name='exchange',
-    )(*rows, stat, logits, tab, lam.reshape(1))
+    )(*rows, logits, tab, lam.reshape(1))
 
 
 def solution(mesh):

time: 56.1 us -> 52.4 us (0.934)
  Pallas kernels: 53.1 us -> 49.4 us
    pallas_call x1, Pallas kernels: 41.5 us -> 37.7 us  [step(): pl.pallas_call(functools.partial(exchange_kernel, n), out_shape=jax.Shape...]
where the time goes in v3:
time: 52.4 us; the launch traced here: 52.2 us
  Pallas kernels  49.4 us (94%)
  local copies, waits for them, and re-layouts  1.47 us (3%)
  between operations  1.31 us (2%)
    pallas_call x1, Pallas kernels, step(): pl.pallas_call(functools.partial(exchange_kernel, n), out_shape=jax.Shape...  37.7 us
    pallas_call x1, Pallas kernels, step(): pl.pallas_call(functools.partial(local_kernel, n), out_shape=tuple((jax.S...  11.7 us
    unnamed x1, local copies, waits for them, and re-layouts  1.47 us

profile of v3, /device:TPU:1, one launch (start us, length us, event | category | flops | bytes accessed | tf_op | source)
XLA Modules:
  0.0 52.2 jit_solution(10251014042854915290)
XLA Ops:
  1.3 11.7 %local_scores.1 = (f32[2,9,16,128]{3,2,1,0:T(8,128)}, f32[2,9,8,128]{3,2,1,0:T(8,128)}, f32[2,9,8,128]{3,2,1,0:T(8,128)}, f32[64,256]{1,0:T(8,128)}, s32[3,4,40,128]{3,2,1,0:T(8,128)}) custom-call(s32[8,128]{1,0:T(8,128)} %bitcast.5, s32[1,129]{1,0:T(1,128)} %bounds_ref.1, f32[1]{0:T(128)} %bitcast.3.tau_ref, bf16[64,4096]{1,0:T(8,128)(2,1)} %hid_hbm.1, ...), custom_call_target="tpu_custom_call" | custom-call | tf_op jit(solution)/shard_map/local_scores/pallas_call | solution.py:431
  13.0 37.7 %exchange.1 = f32[64,256]{1,0:T(8,128)} custom-call(f32[2,9,16,128]{3,2,1,0:T(8,128)} %get-tuple-element.10.own0, f32[2,9,8,128]{3,2,1,0:T(8,128)} %get-tuple-element.11.own1, f32[2,9,8,128]{3,2,1,0:T(8,128)} %get-tuple-element.12.own2, f32[64,256]{1,0:T(8,128)} %get-tuple-element.13.logits, s32[3,4,40,128]{3,2,1,0:T(8,128)} %get-tuple-element.14.own_tab, ...), custom_call_target="tpu_custom_call" | custom-call | tf_op jit(solution)/shard_map/exchange/pallas_call | solution.py:449
  50.7 1.5 %copy.11 = f32[64,256]{1,0:T(8,128)} copy(f32[64,256]{1,0:T(8,128)} %exchange.1) | data formatting | bytes 131072

commit v4 on v3

--- a/solution.py
+++ b/solution.py
@@ -9,7 +9,8 @@
 
 F32, BF16, I32 = jnp.float32, jnp.bfloat16, jnp.int32
 GROUPS = ((0, 16), (16, 8), (24, 8))
-UNROLL = 2
+UNROLL = 4
+AHEAD = 4
 HALF = 32
 LN, EN = 128, 1024
 NT = (((1,), (1,)), ((), ()))
@@ -38,7 +39,7 @@
         rows = pl.ds(c * kchunk, kchunk)
         return pltpu.make_async_copy(keys_hbm.at[rows], keys.at[rows], key_sem.at[c])
 
-    for c in range(nk):
+    for c in range(AHEAD):
         key_copy(c).start()
 
     lane = iota((8, LN), 1)
@@ -70,9 +71,15 @@
         hi_b = jnp.concatenate([hi_b, jnp.zeros((8, LN - nb), I32)], axis=1)
     counted = (pos >= jnp.take_along_axis(lo_b, owner, axis=1)) & (pos < jnp.take_along_axis(hi_b, owner, axis=1))
     rank_d = jnp.where(counted, rank, -1)
+    small = iota((LN, LN), 0).astype(F32).astype(BF16)
+    one, none = jnp.ones((LN, LN), BF16), jnp.zeros((LN, LN), BF16)
+
+    def hot(row, value=one):
+        return jnp.where(jnp.broadcast_to(row.astype(F32).astype(BF16), (LN, LN)) == small, value, none)
+
     for t in range(8):
-        rows = iota((EN, LN), 0)
-        dedup[:, t * LN:(t + 1) * LN] = jnp.where(rank_d[t:t + 1, :] == rows, 1.0, 0.0).astype(BF16)
+        for r in range(8):
+            dedup[r * LN:(r + 1) * LN, t * LN:(t + 1) * LN] = hot(rank_d[t:t + 1, :] - r * LN)
 
     h = tok // LN
     tile_first = ((h != prev(h)) | (pos == 0)).astype(I32)
@@ -87,7 +94,7 @@
     for t in range(8):
         cols = slice(t * LN, (t + 1) * LN)
         r = slice(t, t + 1)
-        lohot[0:LN, cols] = jnp.where(lo[r, :] == iota((LN, LN), 0), val[r, :], 0.0).astype(BF16)
+        lohot[0:LN, cols] = hot(lo[r, :], jnp.broadcast_to(val[r, :].astype(BF16), (LN, LN)))
         lohot[LN:160, cols] = jnp.where(
             sub32 < 8, starts[0][r, :], jnp.where(sub32 < 16, starts[1][r, :], jnp.where(
                 sub32 < 24, starts[2][r, :], starts[3][r, :]))).astype(BF16)
@@ -95,8 +102,7 @@
     for a, (b2, b3) in enumerate(((2, 1), (2, 0), (1, 0))):
         row = ((jp[a] - coord[a] + n) % n) * inner + jp[b2] * (2 * n) + jp[b3] * 2 + jc
         for t in range(8):
-            onehot[:, t * LN:(t + 1) * LN] = jnp.where(
-                row[t:t + 1, :] == iota((LN, LN), 0), 1.0, 0.0).astype(BF16)
+            onehot[:, t * LN:(t + 1) * LN] = hot(row[t:t + 1, :])
         tb = lax.dot_general(onehot[...], lohot[0:LN, :], NT, preferred_element_type=F32).astype(I32)
         us = lax.dot_general(lohot[LN:160, :], onehot[...], NT, preferred_element_type=F32).astype(I32)
         for d in range(n):
@@ -114,8 +120,13 @@
     tau = tau_ref[0]
 
     def score_step(c, carry):
-        key_copy(2 * c).wait()
-        key_copy(2 * c + 1).wait()
+        for i in range(2):
+            key_copy(2 * c + i).wait()
+
+            @pl.when(2 * c + i + AHEAD < nk)
+            def _():
+                key_copy(2 * c + i + AHEAD).start()
+
         rows = pl.ds(c * 256, 256)
         cross = lax.dot_general(hid[...], keys[rows, :], NT, preferred_element_type=F32)
         sq = jnp.zeros((256, LN), F32)
@@ -430,9 +441,9 @@
     hbm = pl.BlockSpec(memory_space=pl.ANY)
     *rows, logits, tab = pl.pallas_call(
         functools.partial(local_kernel, n),
-        out_shape=tuple(jax.ShapeDtypeStruct((2, 9, nr, LN), F32) for _, nr in GROUPS) + (
-            jax.ShapeDtypeStruct((64, 256), F32),
-            jax.ShapeDtypeStruct((3, n, tab_rows, LN), I32)),
+        out_shape=tuple(pltpu.VMEM((2, 9, nr, LN), F32) for _, nr in GROUPS) + (
+            pltpu.VMEM((64, 256), F32),
+            pltpu.VMEM((3, n, tab_rows, LN), I32)),
         in_specs=[vm, vm, sm, hbm, hbm, hbm],
         out_specs=(vm,) * 5,
         scratch_shapes=[
@@ -460,7 +471,7 @@
             DMA((3, m, 2)), DMA((3, m, 2)), DMA((3, 2)), DMA((3, 2)), DMA((3, 2)), DMA((3, 2)), DMA((3, m)), DMA((3, m))],
         compiler_params=pltpu.CompilerParams(collective_id=0, has_side_effects=True),
         name='exchange',
-    )(*rows, logits, tab, lam.reshape(1))
+    )(*[pltpu.with_memory_space_constraint(x, pltpu.VMEM) for x in (*rows, logits, tab)], lam.reshape(1))
 
 
 def solution(mesh):

time: 52.4 us -> 48.7 us (0.929)
  Pallas kernels: 49.4 us -> 45.7 us
    pallas_call x1, Pallas kernels: 37.7 us -> 35.8 us  [step(): pl.pallas_call(functools.partial(exchange_kernel, n), out_shape=jax.Shape...]
    pallas_call x1, Pallas kernels: 11.7 us -> 9.97 us  [step(): pl.pallas_call(functools.partial(local_kernel, n), out_shape=tuple((pltpu...]
where the time goes in v4:
time: 48.7 us; the launch traced here: 48.5 us
  Pallas kernels  45.7 us (94%)
  local copies, waits for them, and re-layouts  1.47 us (3%)
  between operations  1.31 us (3%)
    pallas_call x1, Pallas kernels, step(): pl.pallas_call(functools.partial(exchange_kernel, n), out_shape=jax.Shape...  35.8 us
    pallas_call x1, Pallas kernels, step(): pl.pallas_call(functools.partial(local_kernel, n), out_shape=tuple((pltpu...  9.97 us
    unnamed x1, local copies, waits for them, and re-layouts  1.47 us

profile of v4, /device:TPU:1, one launch (start us, length us, event | category | flops | bytes accessed | tf_op | source)
XLA Modules:
  0.0 48.5 jit_solution(14259374497656460103)
XLA Ops:
  1.3 10.0 %local_scores.1 = (f32[2,9,16,128]{3,2,1,0:T(8,128)S(1)}, f32[2,9,8,128]{3,2,1,0:T(8,128)S(1)}, f32[2,9,8,128]{3,2,1,0:T(8,128)S(1)}, f32[64,256]{1,0:T(8,128)S(1)}, s32[3,4,40,128]{3,2,1,0:T(8,128)S(1)}) custom-call(s32[8,128]{1,0:T(8,128)} %bitcast.5, s32[1,129]{1,0:T(1,128)} %bounds_ref.1, f32[1]{0:T(128)} %bitcast.3.tau_ref, bf16[64,4096]{1,0:T(8,128)(2,1)} %hid_hbm.1, ...), custom_call_target="tpu_custom_call" | custom-call | tf_op jit(solution)/shard_map/local_scores/pallas_call | solution.py:442
  11.3 35.8 %exchange.1 = f32[64,256]{1,0:T(8,128)} custom-call(f32[2,9,16,128]{3,2,1,0:T(8,128)S(1)} %get-tuple-element.10.own0, f32[2,9,8,128]{3,2,1,0:T(8,128)S(1)} %get-tuple-element.11.own1, f32[2,9,8,128]{3,2,1,0:T(8,128)S(1)} %get-tuple-element.12.own2, f32[64,256]{1,0:T(8,128)S(1)} %get-tuple-element.13.logits, s32[3,4,40,128]{3,2,1,0:T(8,128)S(1)} %get-tuple-element.14.own_tab, ...), custom_call_target="tpu_custom_call" | custom-call | tf_op jit(solution)/shard_map/exchange/pallas_call | solution.py:460
  47.0 1.5 %copy.11 = f32[64,256]{1,0:T(8,128)} copy(f32[64,256]{1,0:T(8,128)} %exchange.1) | data formatting | bytes 131072

commit v5 on v4

--- a/solution.py
+++ b/solution.py
@@ -25,12 +25,13 @@
     return device, device % 2, (device // 2) % n, (device // (2 * n)) % n, device // (2 * n * n)
 
 
-def local_kernel(n, tok_ref, bounds_ref, tau_ref, hid_hbm, w_hbm, keys_hbm, rows0, rows1, rows2, logits_out, tab_out,
-                 hid, w, keys, score, dedup, onehot, lohot, e3, in_sem, key_sem):
+def local_kernel(n, tok_hbm, bounds_hbm, tau_hbm, hid_hbm, w_hbm, keys_hbm, rows0, rows1, rows2, logits_out, tab_out,
+                 tok_ref, bounds_ref, tau_ref, hid, w, keys, score, dedup, onehot, lohot, e3, in_sem, key_sem):
     inner = 2 * n * n
     _, _, cx, cy, cz = coordinates(n)
-    in_copies = (pltpu.make_async_copy(hid_hbm, hid, in_sem.at[0]), pltpu.make_async_copy(w_hbm, w, in_sem.at[1]))
-    for c in in_copies:
+    operands = ((tok_hbm, tok_ref), (bounds_hbm, bounds_ref), (tau_hbm, tau_ref), (hid_hbm, hid), (w_hbm, w))
+    in_copies = [pltpu.make_async_copy(a, b, in_sem.at[i]) for i, (a, b) in enumerate(operands)]
+    for c in in_copies[:-1]:
         c.start()
     kchunk = LN
     nk = keys.shape[0] // kchunk
@@ -50,6 +51,7 @@
         r = pltpu.roll(a, 1, 1)
         return jnp.where(lane == 0, pltpu.roll(r, 1, 0), r)
 
+    in_copies[0].wait()
     tok = tok_ref[...]
     first = ((tok != prev(tok)) | (pos == 0)).astype(I32)
     c = first
@@ -62,6 +64,7 @@
     rank = c + acc - tot - 1
 
     owner = tok // 256
+    in_copies[1].wait()
     bnd = bounds_ref[...]
     nb = bnd.shape[1] - 1
     lo_b = jnp.broadcast_to(bnd[:, :nb], (8, nb))
@@ -110,13 +113,9 @@
             for hf in range(2):
                 tab_out[a, d, inner + hf:inner + hf + 1, :] = us[16 * hf:16 * hf + 1] * LN + us[16 * hf + 8:16 * hf + 9]
 
-    for c in in_copies:
+    in_copies[-1].start()
+    for c in in_copies[2:-1]:
         c.wait()
-    lg = jnp.dot(hid[...], w[...], preferred_element_type=F32)
-    logits_out[...] = lg
-    lm = jnp.max(lg, axis=1, keepdims=True)
-    lz = jnp.sum(jnp.exp(lg - lm), axis=1, keepdims=True)
-
     tau = tau_ref[0]
 
     def score_step(c, carry):
@@ -140,6 +139,12 @@
         return carry
 
     lax.fori_loop(0, nk // 2, score_step, 0)
+
+    in_copies[-1].wait()
+    lg = jnp.dot(hid[...], w[...], preferred_element_type=F32)
+    logits_out[...] = lg
+    lm = jnp.max(lg, axis=1, keepdims=True)
+    lz = jnp.sum(jnp.exp(lg - lm), axis=1, keepdims=True)
 
     sc = [score[t] for t in range(8)]
     m = jnp.max(functools.reduce(jnp.maximum, sc), axis=1, keepdims=True)
@@ -171,10 +176,10 @@
                     out[h, 2 * c + t] = eu[h * HALF + r0:h * HALF + r0 + nr, t * LN:(t + 1) * LN]
 
 
-def exchange_kernel(n, own0, own1, own2, logits, own_tab, lam_ref, out_ref,
-                    tab_pair, tab, tab_smem, list0, list1, list2, scaled0, scaled1, scaled2,
+def exchange_kernel(n, own0, own1, own2, own_tab, lam_hbm, hist_out, stat_out,
+                    lam_ref, lam_sem, tab_pair, tab, tab_smem, list0, list1, list2, scaled0, scaled1, scaled2,
                     part20, part21, part22, relay0, relay1, relay2, recv20, recv21, recv22,
-                    part30, part31, part32, recv30, recv31, recv32, fin, fin_in,
+                    part30, part31, part32, recv30, recv31, recv32,
                     swap_sem, tab_send, tab_recv, smem_sem,
                     send1, recv1, send2, recv2_sem, send_relay, recv_relay, send3, recv3_sem):
     inner = 2 * n * n
@@ -221,6 +226,8 @@
         c.start()
         sends.append(c)
 
+    lam_copy = pltpu.make_async_copy(lam_hbm, lam_ref, lam_sem)
+    lam_copy.start()
     barrier = pltpu.get_barrier_semaphore()
     partners = [partner] + [axis_peer(start, a, d) for start in (device, partner) for a in range(3) for d in range(1, n)]
     for p in partners:
@@ -344,9 +351,9 @@
         return remote(part2[g].at[2, halves[i]], relay[g].at[i], send_relay.at[g, i], recv_relay.at[g, i],
                       peer((g + 1) % 3, near[i]))
 
-    def copy3(g, d):
-        return remote(part3[g].at[d], recv3[g].at[n - d - 1], send3.at[g, d - 1], recv3_sem.at[g, n - d - 1],
-                      peer((g + 2) % 3, d))
+    def copy3(g, d, l):
+        return remote(part3[g].at[d, other if l else core], recv3[g].at[n - d - 1, l], send3.at[g, d, l],
+                      recv3_sem.at[g, n - d - 1, l], peer((g + 2) % 3, d) + l * (partner - device))
 
     group_stat = {}
     for g in order:
@@ -367,7 +374,6 @@
     for g in order:
         for d2 in near:
             partial_hist(g, d2)
-    for g in order:
         for i, d2 in enumerate(near):
             if far:
                 copy2_relay(g, i).wait_recv()
@@ -395,40 +401,35 @@
             for ch in range(4):
                 q = d3 * 4 + ch
                 q = q + q // mid
-                part3[g][d3, ch] = sum(p[q] * f for p, f in zip(parts, fs))
-            part3[g][d3, 4] = tile
-            if d3:
-                go(copy3(g, d3))
-
-    for g in order:
-        r0, nr = GROUPS[g]
-        for d in range(1, n):
-            copy3(g, d).wait_recv()
-        parts = [part3[g].at[0]] + [recv3[g].at[k] for k in range(n - 1)]
-        fs, tile = stats([p[4] for p in parts])
-        for ch in range(4):
-            fin[ch // 2, ch % 2, r0:r0 + nr] = sum(p[ch] * f for p, f in zip(parts, fs))
-        for c in range(2):
-            fin[c, 2, r0:r0 + nr] = tile
-
-    back = remote(fin.at[other], fin_in, swap_sem.at[0, 4], swap_sem.at[1, 4], partner)
-    go(back)
-    lam = lam_ref[0]
-
-    def finish(block_ref, rows_half):
-        st = block_ref[2]
-        zz, ll, lzz = st[:, 1:2], st[:, 2:3], st[:, 3:4]
-        rows = pl.ds(pl.multiple_of(rows_half * HALF, 8), HALF)
-        for hf in range(2):
-            cols = slice(hf * LN, (hf + 1) * LN)
-            lm_exp = jnp.exp(logits[rows, cols] - ll)
-            out_ref[rows, cols] = jnp.log(lam * (block_ref[hf] / zz) + (1.0 - lam) * (lm_exp / lzz))
-
-    finish(fin.at[core], core)
-    back.wait_recv()
-    finish(fin_in, other)
+                part3[g][d3, ch // 2, ch % 2] = sum(p[q] * f for p, f in zip(parts, fs))
+            for c in range(2):
+                part3[g][d3, c, 2] = tile
+            for l in range(2):
+                if d3 or l:
+                    go(copy3(g, d3, l))
+
+    lam_copy.wait()
+    for l in range(2):
+        for g in order:
+            r0, nr = GROUPS[g]
+            for d in range(l == 0, n):
+                copy3(g, d, l).wait_recv()
+            parts = [recv3[g].at[k, l] for k in range(n - 1)] + [recv3[g].at[n - 1, 1] if l else part3[g].at[0, core]]
+            fs, tile = stats([p[2] for p in parts])
+            rows = pl.ds(pl.multiple_of((other if l else core) * HALF + r0, 8), nr)
+            for hf in range(2):
+                hist_out[hf, rows] = sum(p[hf] * f for p, f in zip(parts, fs))
+            stat_out[rows] = jnp.where(iota((nr, LN), 1) == 4, lam_ref[0], tile)
     for c in sends:
         c.wait_send()
+
+
+def mixture_kernel(hist, stat, logits, out_ref):
+    zz, ll, lzz, lam = (stat[:, i:i + 1] for i in range(1, 5))
+    for hf in range(2):
+        cols = slice(hf * LN, (hf + 1) * LN)
+        lm_exp = jnp.exp(logits[:, cols] - ll)
+        out_ref[:, cols] = jnp.log(lam * (hist[hf] / zz) + (1.0 - lam) * (lm_exp / lzz))
 
 
 def step(n, hidden, w_local, keys_local, tok_local, bounds_local, tau, lam):
@@ -437,41 +438,47 @@
     dim = hidden.shape[1]
     V, DMA = pltpu.VMEM, pltpu.SemaphoreType.DMA
     vm = pl.BlockSpec(memory_space=pltpu.VMEM)
-    sm = pl.BlockSpec(memory_space=pltpu.SMEM)
     hbm = pl.BlockSpec(memory_space=pl.ANY)
     *rows, logits, tab = pl.pallas_call(
         functools.partial(local_kernel, n),
         out_shape=tuple(pltpu.VMEM((2, 9, nr, LN), F32) for _, nr in GROUPS) + (
             pltpu.VMEM((64, 256), F32),
             pltpu.VMEM((3, n, tab_rows, LN), I32)),
-        in_specs=[vm, vm, sm, hbm, hbm, hbm],
+        in_specs=[hbm] * 6,
         out_specs=(vm,) * 5,
         scratch_shapes=[
-            V((64, dim), BF16), V((dim, 256), BF16), V((EN, dim), BF16), V((8, 64, LN), F32),
+            V((8, LN), I32), V(bounds_local.shape, I32), pltpu.SMEM((1,), F32), V((64, dim), BF16), V((dim, 256), BF16), V((EN, dim), BF16), V((8, 64, LN), F32),
             V((EN, EN), BF16), V((LN, EN), BF16), V((160, EN), BF16), V((192, EN), BF16),
-            DMA((2,)), DMA((8,))],
+            DMA((5,)), DMA((8,))],
         name='local_scores',
     )(tok_local.reshape(8, LN), bounds_local, tau.reshape(1), hidden, w_local, keys_local)
 
     def per_group(*lead):
         return [V((*lead, nr, LN), F32) for _, nr in GROUPS]
 
+    def in_vmem(*arrays):
+        return [pltpu.with_memory_space_constraint(x, pltpu.VMEM) for x in arrays]
+
     m = n - 1
-    return pl.pallas_call(
+    hist, stat = pl.pallas_call(
         functools.partial(exchange_kernel, n),
-        out_shape=jax.ShapeDtypeStruct((64, 256), F32),
-        in_specs=[vm] * 5 + [sm],
-        out_specs=vm,
+        out_shape=(V((2, 64, LN), F32), V((64, LN), F32)),
+        in_specs=[vm] * 4 + [hbm],
+        out_specs=(vm, vm),
         scratch_shapes=[
-            V((3, tab_rows, LN), I32), V((3, m, 2, tab_rows, LN), I32), pltpu.SMEM((3, n, 2, 2, LN), I32),
+            pltpu.SMEM((1,), F32), DMA(()), V((3, tab_rows, LN), I32), V((3, m, 2, tab_rows, LN), I32),
+            pltpu.SMEM((3, n, 2, 2, LN), I32),
             *per_group(2 * n - 1, 9), *per_group(2 * n, 9), *per_group(n, block + 1), *per_group(2, block // 2 + 1),
-            *per_group(2, block + 1), *per_group(n, 5), *per_group(m, 5),
-            V((2, 3, HALF, LN), F32), V((3, HALF, LN), F32),
-            DMA((2, 5)), DMA((3, m, 2)), DMA((3, m, 2)), DMA((3, n, 2)),
-            DMA((3, m, 2)), DMA((3, m, 2)), DMA((3, 2)), DMA((3, 2)), DMA((3, 2)), DMA((3, 2)), DMA((3, m)), DMA((3, m))],
+            *per_group(2, block + 1), *per_group(n, 2, 3), *per_group(n, 2, 3),
+            DMA((2, 4)), DMA((3, m, 2)), DMA((3, m, 2)), DMA((3, n, 2)),
+            DMA((3, m, 2)), DMA((3, m, 2)), DMA((3, 2)), DMA((3, 2)), DMA((3, 2)), DMA((3, 2)),
+            DMA((3, n, 2)), DMA((3, n, 2))],
         compiler_params=pltpu.CompilerParams(collective_id=0, has_side_effects=True),
         name='exchange',
-    )(*[pltpu.with_memory_space_constraint(x, pltpu.VMEM) for x in (*rows, logits, tab)], lam.reshape(1))
+    )(*in_vmem(*rows, tab), lam.reshape(1))
+    return pl.pallas_call(
+        mixture_kernel, out_shape=jax.ShapeDtypeStruct((64, 256), F32), in_specs=[vm] * 3, out_specs=vm, name='mixture',
+    )(*in_vmem(hist, stat, logits))
 
 
 def solution(mesh):

time: 48.7 us -> 44.5 us (0.914)
  Pallas kernels: 45.7 us -> 43.1 us
  local copies, waits for them, and re-layouts: 1.47 us -> 0 us
    pallas_call x1, Pallas kernels: 9.97 us -> 7.88 us  [step(): pl.pallas_call(functools.partial(local_kernel, n), out_shape=tuple((pltpu...]
    unnamed x1 -> x0, local copies, waits for them, and re-layouts: 1.47 us -> none
    pallas_call x1 -> x2, Pallas kernels: 35.8 us -> 35.2 us  [the longest x1 34.4 us: step(): pl.pallas_call(functools.partial(exchange_kernel, n), out_shape=(V((2, 64...]
where the time goes in v5:
time: 44.5 us; the launch traced here: 44.4 us
  Pallas kernels  43.1 us (97%)
  between operations  1.31 us (3%)
    pallas_call x1, Pallas kernels, step(): pl.pallas_call(functools.partial(exchange_kernel, n), out_shape=(V((2, 64...  34.4 us
    pallas_call x1, Pallas kernels, step(): pl.pallas_call(functools.partial(local_kernel, n), out_shape=tuple((pltpu...  7.88 us

profile of v5, /device:TPU:1, one launch (start us, length us, event | category | flops | bytes accessed | tf_op | source)
XLA Modules:
  0.0 44.4 jit_solution(13164309277661761971)
XLA Ops:
  1.3 7.9 %local_scores.1 = (f32[2,9,16,128]{3,2,1,0:T(8,128)S(1)}, f32[2,9,8,128]{3,2,1,0:T(8,128)S(1)}, f32[2,9,8,128]{3,2,1,0:T(8,128)S(1)}, f32[64,256]{1,0:T(8,128)S(1)}, s32[3,4,40,128]{3,2,1,0:T(8,128)S(1)}) custom-call(s32[8,128]{1,0:T(8,128)} %bitcast.5, s32[1,129]{1,0:T(1,128)} %bounds_hbm.1, f32[1]{0:T(128)} %bitcast.3.tau_hbm, bf16[64,4096]{1,0:T(8,128)(2,1)} %hid_hbm.1, ...), custom_call_target="tpu_custom_call" | custom-call | tf_op jit(solution)/shard_map/local_scores/pallas_call | solution.py:442
  9.2 34.4 %exchange.1 = (f32[2,64,128]{2,1,0:T(8,128)S(1)}, f32[64,128]{1,0:T(8,128)S(1)}) custom-call(f32[2,9,16,128]{3,2,1,0:T(8,128)S(1)} %get-tuple-element.12.own0, f32[2,9,8,128]{3,2,1,0:T(8,128)S(1)} %get-tuple-element.13.own1, f32[2,9,8,128]{3,2,1,0:T(8,128)S(1)} %get-tuple-element.14.own2, s32[3,4,40,128]{3,2,1,0:T(8,128)S(1)} %get-tuple-element.15.own_tab, ...), custom_call_target="tpu_custom_call" | custom-call | tf_op jit(solution)/shard_map/exchange/pallas_call | solution.py:463
  43.6 0.8 %mixture.1 = f32[64,256]{1,0:T(8,128)} custom-call(f32[2,64,128]{2,1,0:T(8,128)S(1)} %get-tuple-element.16.hist, f32[64,128]{1,0:T(8,128)S(1)} %get-tuple-element.17.stat, f32[64,256]{1,0:T(8,128)S(1)} %get-tuple-element.18.logits), custom_call_target="tpu_custom_call" | custom-call | tf_op jit(solution)/shard_map/mixture/pallas_call | solution.py:479

commit v6 on v5

--- a/solution.py
+++ b/solution.py
@@ -241,9 +241,13 @@
     row_swap = [remote(own[g].at[other], lists[g].at[0], swap_sem.at[0, 1 + g], swap_sem.at[1, 1 + g], partner)
                 for g in range(3)]
 
-    def tab_copy(a, d, l):
-        return remote(own_tab.at[a, d], tab.at[a, n - d - 1, l], tab_send.at[a, d - 1, l], tab_recv.at[a, n - d - 1, l],
-                      axis_peer(partner if l else device, a, d))
+    def tab_copy(a, d):
+        return remote(own_tab.at[a, d], tab.at[a, n - d - 1, 0], tab_send.at[a, d - 1, 0], tab_recv.at[a, n - d - 1, 0],
+                      axis_peer(device, a, d))
+
+    def tab_share(a, d):
+        i = n - d - 1
+        return remote(tab.at[a, i, 0], tab.at[a, i, 1], tab_send.at[a, i, 1], tab_recv.at[a, i, 1], partner)
 
     def row_copy(g, d, l):
         return remote(own[g].at[other if l else core], lists[g].at[2 * (n - d) - 1 + l], send1.at[g, d - 1, l],
@@ -253,17 +257,18 @@
         frm, to = (n - 1, 1) if l == 0 else (1, n - 1)
         return remote(lists[g].at[2 * frm - 1 + l], lists[g].at[3 + l], send1.at[g, 1, l], recv1.at[g, 1, l], peer(g, to))
 
-    for g in order:
-        for d in near:
-            for l in range(2):
+    onward = [(d, l) for l, d in enumerate(near)]
+    rest = [(d, l) for d in near for l in range(2) if (d, l) not in onward]
+    for pairs in (onward, rest):
+        for g in order:
+            for d, l in pairs:
                 go(row_copy(g, d, l))
     for g in order:
         go(row_swap[g])
     go(tab_swap)
     for d in far + near:
         for a in range(3):
-            for l in range(2):
-                go(tab_copy(a, d, l))
+            go(tab_copy(a, d))
 
     def stats(tiles, counted=None):
         shape = tiles[0].shape
@@ -279,13 +284,10 @@
         return fs, jnp.where(ln == 0, mm, jnp.where(ln == 1, zz, jnp.where(ln == 2, ll, lzz)))
 
     for g in order:
-        for d in near:
-            for l in range(2):
-                row_copy(g, d, l).wait_recv()
         if far:
             for l in range(2):
+                row_copy(g, near[l], l).wait_recv()
                 go(row_relay(g, l))
-        row_swap[g].wait_recv()
 
     def tab_of(a, k, l):
         if k:
@@ -297,11 +299,14 @@
             return own[g].at[core]
         return lists[g].at[2 * k - 1 + l]
 
+    for d in near + far:
+        for a in range(3):
+            tab_copy(a, d).wait_recv()
+            go(tab_share(a, d))
     tab_swap.wait_recv()
-    for d in range(1, n):
-        for l in range(2):
-            for a in range(3):
-                tab_copy(a, d, l).wait_recv()
+    for d in near + far:
+        for a in range(3):
+            tab_share(a, d).wait_recv()
     smem_copies = [pltpu.make_async_copy(tab_of(axis_of[g], k, l).at[pl.ds(inner, 2)], tab_smem.at[g, k, l],
                                          smem_sem.at[g, k, l])
                    for g in range(3) for k in range(n) for l in range(2)]
@@ -334,18 +339,19 @@
                     code = lax.shift_right_logical(packed, 8) if hf else packed
                     got = jnp.take_along_axis(merged, code & 127, axis=1, mode='promise_in_bounds')
                     acc[hf] = acc[hf] + jnp.where((code & LN) != 0, got, 0.0)
-            t = 2 * q + lax.div(q, n)
+            t = 2 * q + 2 * lax.div(q, n)
             part2[g][d2, t] = acc[0]
             part2[g][d2, t + 1] = acc[1]
             return carry
 
         lax.fori_loop(0, mid, pair_step, 0, unroll=UNROLL)
 
-    halves = (pl.ds(0, mid + 1), pl.ds(mid, mid + 1))
-
-    def copy2(g, d):
-        i = 0 if d == 1 else 1
-        return remote(part2[g].at[d], recv2[g].at[i], send2.at[g, i], recv2_sem.at[g, i], peer((g + 1) % 3, d))
+    halves = (pl.ds(0, mid + 1), pl.ds(mid + 1, mid + 1))
+    stat_at = (mid, 0)
+
+    def copy2(g, i, h):
+        return remote(part2[g].at[near[i], halves[h]], recv2[g].at[i, h], send2.at[g, i, h], recv2_sem.at[g, i, h],
+                      peer((g + 1) % 3, near[i]))
 
     def copy2_relay(g, i):
         return remote(part2[g].at[2, halves[i]], relay[g].at[i], send_relay.at[g, i], recv_relay.at[g, i],
@@ -357,6 +363,9 @@
 
     group_stat = {}
     for g in order:
+        row_swap[g].wait_recv()
+        for d, l in rest if far else onward + rest:
+            row_copy(g, d, l).wait_recv()
         if far:
             for l in range(2):
                 row_relay(g, l).wait_recv()
@@ -366,42 +375,44 @@
             for t in range(8):
                 scaled[g][i, t] = rows[t] * fs[i]
         for d2 in far + near + (0,):
-            part2[g][d2, mid] = group_stat[g]
+            for h in range(2):
+                part2[g][d2, mid + h] = group_stat[g]
         for d2 in far:
             partial_hist(g, d2)
             for i in range(2):
                 go(copy2_relay(g, i))
     for g in order:
-        for d2 in near:
+        for i, d2 in enumerate(near):
             partial_hist(g, d2)
+            go(copy2(g, i, 1 - i))
         for i, d2 in enumerate(near):
             if far:
                 copy2_relay(g, i).wait_recv()
-                there = relay[g][i, 0 if i else mid]
+                there = relay[g][i, stat_at[i]]
                 zero = jnp.zeros(there.shape, F32)
                 fs, tile = stats([group_stat[g], there], [group_stat[g], zero if i else there])
-                for t in range(block + 1):
-                    r = t - i * mid
-                    if t == mid:
-                        part2[g][d2, t] = tile
-                    elif 0 <= r <= mid:
-                        part2[g][d2, t] = part2[g][d2, t] * fs[0] + relay[g][i, r] * fs[1]
-                    else:
-                        part2[g][d2, t] = part2[g][d2, t] * fs[0]
-            go(copy2(g, d2))
+                for t in range(mid + 1):
+                    r = t + i * (mid + 1)
+                    part2[g][d2, r] = tile if t == stat_at[i] else part2[g][d2, r] * fs[0] + relay[g][i, t] * fs[1]
+            go(copy2(g, i, i))
     for g in order:
         partial_hist(g, 0)
 
     for g in order:
-        for d in near:
-            copy2(g, d).wait_recv()
-        parts = [part2[g].at[0]] + [recv2[g].at[i] for i in range(len(near))]
-        fs, tile = stats([p[mid] for p in parts])
+        for i in range(len(near)):
+            for h in range(2):
+                copy2(g, i, h).wait_recv()
+        keys2 = [(i, (i + j) % 2) for j in range(2) for i in range(len(near))]
+        there = [recv2[g][i, h, stat_at[h]] for i, h in keys2]
+        zero = jnp.zeros(there[0].shape, F32)
+        fs, tile = stats([group_stat[g]] + there, [group_stat[g]] + there[:len(near)] + [zero] * len(near))
+        factor = dict(zip(keys2, fs[1:]))
         for d3 in far + near + (0,):
             for ch in range(4):
                 q = d3 * 4 + ch
-                q = q + q // mid
-                part3[g][d3, ch // 2, ch % 2] = sum(p[q] * f for p, f in zip(parts, fs))
+                h = q // mid
+                part3[g][d3, ch // 2, ch % 2] = part2[g][0, q + 2 * h] * fs[0] + sum(
+                    recv2[g][i, h, q % mid + h] * factor[i, h] for i in range(len(near)))
             for c in range(2):
                 part3[g][d3, c, 2] = tile
             for l in range(2):
@@ -468,10 +479,10 @@
         scratch_shapes=[
             pltpu.SMEM((1,), F32), DMA(()), V((3, tab_rows, LN), I32), V((3, m, 2, tab_rows, LN), I32),
             pltpu.SMEM((3, n, 2, 2, LN), I32),
-            *per_group(2 * n - 1, 9), *per_group(2 * n, 9), *per_group(n, block + 1), *per_group(2, block // 2 + 1),
-            *per_group(2, block + 1), *per_group(n, 2, 3), *per_group(n, 2, 3),
+            *per_group(2 * n - 1, 9), *per_group(2 * n, 9), *per_group(n, block + 2), *per_group(2, block // 2 + 1),
+            *per_group(2, 2, block // 2 + 1), *per_group(n, 2, 3), *per_group(n, 2, 3),
             DMA((2, 4)), DMA((3, m, 2)), DMA((3, m, 2)), DMA((3, n, 2)),
-            DMA((3, m, 2)), DMA((3, m, 2)), DMA((3, 2)), DMA((3, 2)), DMA((3, 2)), DMA((3, 2)),
+            DMA((3, m, 2)), DMA((3, m, 2)), DMA((3, 2, 2)), DMA((3, 2, 2)), DMA((3, 2)), DMA((3, 2)),
             DMA((3, n, 2)), DMA((3, n, 2))],
         compiler_params=pltpu.CompilerParams(collective_id=0, has_side_effects=True),
         name='exchange',

time: 44.5 us -> 42.4 us (0.953)
  Pallas kernels: 43.1 us -> 41 us
    pallas_call x1, Pallas kernels: 34.4 us -> 32.4 us  [step(): pl.pallas_call(functools.partial(exchange_kernel, n), out_shape=(V((2, 64...]
where the time goes in v6:
time: 42.4 us; the launch traced here: 42.3 us
  Pallas kernels  41 us (97%)
  between operations  1.31 us (3%)
    pallas_call x1, Pallas kernels, step(): pl.pallas_call(functools.partial(exchange_kernel, n), out_shape=(V((2, 64...  32.4 us
    pallas_call x1, Pallas kernels, step(): pl.pallas_call(functools.partial(local_kernel, n), out_shape=tuple((pltpu...  7.88 us

profile of v6, /device:TPU:1, one launch (start us, length us, event | category | flops | bytes accessed | tf_op | source)
XLA Modules:
  0.0 42.3 jit_solution(1014945089374716024)
XLA Ops:
  1.3 7.9 %local_scores.1 = (f32[2,9,16,128]{3,2,1,0:T(8,128)S(1)}, f32[2,9,8,128]{3,2,1,0:T(8,128)S(1)}, f32[2,9,8,128]{3,2,1,0:T(8,128)S(1)}, f32[64,256]{1,0:T(8,128)S(1)}, s32[3,4,40,128]{3,2,1,0:T(8,128)S(1)}) custom-call(s32[8,128]{1,0:T(8,128)} %bitcast.5, s32[1,129]{1,0:T(1,128)} %bounds_hbm.1, f32[1]{0:T(128)} %bitcast.3.tau_hbm, bf16[64,4096]{1,0:T(8,128)(2,1)} %hid_hbm.1, ...), custom_call_target="tpu_custom_call" | custom-call | tf_op jit(solution)/shard_map/local_scores/pallas_call | solution.py:453
  9.2 32.4 %exchange.1 = (f32[2,64,128]{2,1,0:T(8,128)S(1)}, f32[64,128]{1,0:T(8,128)S(1)}) custom-call(f32[2,9,16,128]{3,2,1,0:T(8,128)S(1)} %get-tuple-element.12.own0, f32[2,9,8,128]{3,2,1,0:T(8,128)S(1)} %get-tuple-element.13.own1, f32[2,9,8,128]{3,2,1,0:T(8,128)S(1)} %get-tuple-element.14.own2, s32[3,4,40,128]{3,2,1,0:T(8,128)S(1)} %get-tuple-element.15.own_tab, ...), custom_call_target="tpu_custom_call" | custom-call | tf_op jit(solution)/shard_map/exchange/pallas_call | solution.py:474
  41.6 0.8 %mixture.1 = f32[64,256]{1,0:T(8,128)} custom-call(f32[2,64,128]{2,1,0:T(8,128)S(1)} %get-tuple-element.16.hist, f32[64,128]{1,0:T(8,128)S(1)} %get-tuple-element.17.stat, f32[64,256]{1,0:T(8,128)S(1)} %get-tuple-element.18.logits), custom_call_target="tpu_custom_call" | custom-call | tf_op jit(solution)/shard_map/mixture/pallas_call | solution.py:490

commit v7 on v6

--- a/solution.py
+++ b/solution.py
@@ -25,8 +25,8 @@
     return device, device % 2, (device // 2) % n, (device // (2 * n)) % n, device // (2 * n * n)
 
 
-def local_kernel(n, tok_hbm, bounds_hbm, tau_hbm, hid_hbm, w_hbm, keys_hbm, rows0, rows1, rows2, logits_out, tab_out,
-                 tok_ref, bounds_ref, tau_ref, hid, w, keys, score, dedup, onehot, lohot, e3, in_sem, key_sem):
+def local_kernel(n, tok_hbm, bounds_hbm, tau_hbm, hid_hbm, w_hbm, keys_hbm, score, dedup, logits_out, tab_out,
+                 tok_ref, bounds_ref, tau_ref, hid, w, keys, onehot, lohot, in_sem, key_sem):
     inner = 2 * n * n
     _, _, cx, cy, cz = coordinates(n)
     operands = ((tok_hbm, tok_ref), (bounds_hbm, bounds_ref), (tau_hbm, tau_ref), (hid_hbm, hid), (w_hbm, w))
@@ -143,40 +143,9 @@
     in_copies[-1].wait()
     lg = jnp.dot(hid[...], w[...], preferred_element_type=F32)
     logits_out[...] = lg
-    lm = jnp.max(lg, axis=1, keepdims=True)
-    lz = jnp.sum(jnp.exp(lg - lm), axis=1, keepdims=True)
-
-    sc = [score[t] for t in range(8)]
-    m = jnp.max(functools.reduce(jnp.maximum, sc), axis=1, keepdims=True)
-    z = jnp.zeros((64, LN), F32)
-    for t in range(8):
-        e = jnp.exp(sc[t] - m)
-        z = z + e
-        hi = e.astype(BF16)
-        r1 = e - hi.astype(F32)
-        mid = r1.astype(BF16)
-        low = (r1 - mid.astype(F32)).astype(BF16)
-        cols = slice(t * LN, (t + 1) * LN)
-        e3[0:64, cols] = hi
-        e3[64:LN, cols] = mid
-        e3[LN:192, cols] = low
-    z = jnp.sum(z, axis=1, keepdims=True)
-    l64 = iota((64, LN), 1)
-    stat = jnp.where(l64 == 0, m, jnp.where(l64 == 1, z, jnp.where(l64 == 2, lm, lz)))
-    row_outs = (rows0, rows1, rows2)
-    for h in range(2):
-        for out, (r0, nr) in zip(row_outs, GROUPS):
-            out[h, 8] = stat[h * HALF + r0:h * HALF + r0 + nr]
-    for c in range(4):
-        dd = lax.dot_general(e3[...], dedup[c * 256:(c + 1) * 256, :], NT, preferred_element_type=F32)
-        eu = dd[0:64] + (dd[64:LN] + dd[LN:192])
-        for h in range(2):
-            for out, (r0, nr) in zip(row_outs, GROUPS):
-                for t in range(2):
-                    out[h, 2 * c + t] = eu[h * HALF + r0:h * HALF + r0 + nr, t * LN:(t + 1) * LN]
-
-
-def exchange_kernel(n, own0, own1, own2, own_tab, lam_hbm, hist_out, stat_out,
+
+
+def exchange_kernel(n, score, dedup, logits, own_tab, lam_hbm, hist_out, stat_out, e3, own0, own1, own2,
                     lam_ref, lam_sem, tab_pair, tab, tab_smem, list0, list1, list2, scaled0, scaled1, scaled2,
                     part20, part21, part22, relay0, relay1, relay2, recv20, recv21, recv22,
                     part30, part31, part32, recv30, recv31, recv32,
@@ -235,6 +204,36 @@
     for g in range(3):
         for i in range(2 * n):
             scaled[g][i, 8] = jnp.zeros(scaled[g].shape[2:], F32)
+    lg = logits[...]
+    lm = jnp.max(lg, axis=1, keepdims=True)
+    lz = jnp.sum(jnp.exp(lg - lm), axis=1, keepdims=True)
+    sc = [score[t] for t in range(8)]
+    m = jnp.max(functools.reduce(jnp.maximum, sc), axis=1, keepdims=True)
+    z = jnp.zeros((64, LN), F32)
+    for t in range(8):
+        e = jnp.exp(sc[t] - m)
+        z = z + e
+        hi = e.astype(BF16)
+        r1 = e - hi.astype(F32)
+        middle = r1.astype(BF16)
+        low = (r1 - middle.astype(F32)).astype(BF16)
+        cols = slice(t * LN, (t + 1) * LN)
+        e3[0:64, cols] = hi
+        e3[64:LN, cols] = middle
+        e3[LN:192, cols] = low
+    z = jnp.sum(z, axis=1, keepdims=True)
+    l64 = iota((64, LN), 1)
+    stat = jnp.where(l64 == 0, m, jnp.where(l64 == 1, z, jnp.where(l64 == 2, lm, lz)))
+    for h in range(2):
+        for out, (r0, nr) in zip(own, GROUPS):
+            out[h, 8] = stat[h * HALF + r0:h * HALF + r0 + nr]
+    for c in range(4):
+        dd = lax.dot_general(e3[...], dedup[c * 256:(c + 1) * 256, :], NT, preferred_element_type=F32)
+        eu = dd[0:64] + (dd[64:LN] + dd[LN:192])
+        for h in range(2):
+            for out, (r0, nr) in zip(own, GROUPS):
+                for t in range(2):
+                    out[h, 2 * c + t] = eu[h * HALF + r0:h * HALF + r0 + nr, t * LN:(t + 1) * LN]
     pl.semaphore_wait(barrier, len(partners))
 
     tab_swap = remote(own_tab.at[:, 0], tab_pair, swap_sem.at[0, 0], swap_sem.at[1, 0], partner)
@@ -450,16 +449,15 @@
     V, DMA = pltpu.VMEM, pltpu.SemaphoreType.DMA
     vm = pl.BlockSpec(memory_space=pltpu.VMEM)
     hbm = pl.BlockSpec(memory_space=pl.ANY)
-    *rows, logits, tab = pl.pallas_call(
+    score, dedup, logits, tab = pl.pallas_call(
         functools.partial(local_kernel, n),
-        out_shape=tuple(pltpu.VMEM((2, 9, nr, LN), F32) for _, nr in GROUPS) + (
-            pltpu.VMEM((64, 256), F32),
-            pltpu.VMEM((3, n, tab_rows, LN), I32)),
+        out_shape=(V((8, 64, LN), F32), V((EN, EN), BF16), V((64, 256), F32),
+                   V((3, n, tab_rows, LN), I32)),
         in_specs=[hbm] * 6,
-        out_specs=(vm,) * 5,
+        out_specs=(vm,) * 4,
         scratch_shapes=[
-            V((8, LN), I32), V(bounds_local.shape, I32), pltpu.SMEM((1,), F32), V((64, dim), BF16), V((dim, 256), BF16), V((EN, dim), BF16), V((8, 64, LN), F32),
-            V((EN, EN), BF16), V((LN, EN), BF16), V((160, EN), BF16), V((192, EN), BF16),
+            V((8, LN), I32), V(bounds_local.shape, I32), pltpu.SMEM((1,), F32), V((64, dim), BF16), V((dim, 256), BF16), V((EN, dim), BF16),
+            V((LN, EN), BF16), V((160, EN), BF16),
             DMA((5,)), DMA((8,))],
         name='local_scores',
     )(tok_local.reshape(8, LN), bounds_local, tau.reshape(1), hidden, w_local, keys_local)
@@ -477,7 +475,7 @@
         in_specs=[vm] * 4 + [hbm],
         out_specs=(vm, vm),
         scratch_shapes=[
-            pltpu.SMEM((1,), F32), DMA(()), V((3, tab_rows, LN), I32), V((3, m, 2, tab_rows, LN), I32),
+            V((192, EN), BF16), *per_group(2, 9), pltpu.SMEM((1,), F32), DMA(()), V((3, tab_rows, LN), I32), V((3, m, 2, tab_rows, LN), I32),
             pltpu.SMEM((3, n, 2, 2, LN), I32),
             *per_group(2 * n - 1, 9), *per_group(2 * n, 9), *per_group(n, block + 2), *per_group(2, block // 2 + 1),
             *per_group(2, 2, block // 2 + 1), *per_group(n, 2, 3), *per_group(n, 2, 3),
@@ -486,7 +484,7 @@
             DMA((3, n, 2)), DMA((3, n, 2))],
         compiler_params=pltpu.CompilerParams(collective_id=0, has_side_effects=True),
         name='exchange',
-    )(*in_vmem(*rows, tab), lam.reshape(1))
+    )(*in_vmem(score, dedup, logits, tab), lam.reshape(1))
     return pl.pallas_call(
         mixture_kernel, out_shape=jax.ShapeDtypeStruct((64, 256), F32), in_specs=[vm] * 3, out_specs=vm, name='mixture',
     )(*in_vmem(hist, stat, logits))

time: 42.4 us -> 41.8 us (0.986)
  Pallas kernels: 41 us -> 40.4 us
    pallas_call x1, Pallas kernels: 7.88 us -> 7.26 us  [step(): pl.pallas_call(functools.partial(local_kernel, n), out_shape=(V((8, 64, L...]
where the time goes in v7:
time: 41.8 us; the launch traced here: 41.7 us
  Pallas kernels  40.4 us (97%)
  between operations  1.31 us (3%)
    pallas_call x1, Pallas kernels, step(): pl.pallas_call(functools.partial(exchange_kernel, n), out_shape=(V((2, 64...  32.4 us
    pallas_call x1, Pallas kernels, step(): pl.pallas_call(functools.partial(local_kernel, n), out_shape=(V((8, 64, L...  7.26 us

profile of v7, /device:TPU:1, one launch (start us, length us, event | category | flops | bytes accessed | tf_op | source)
XLA Modules:
  0.0 41.7 jit_solution(4965415183856339856)
XLA Ops:
  1.3 7.3 %local_scores.1 = (f32[8,64,128]{2,1,0:T(8,128)S(1)}, bf16[1024,1024]{1,0:T(8,128)(2,1)S(1)}, f32[64,256]{1,0:T(8,128)S(1)}, s32[3,4,40,128]{3,2,1,0:T(8,128)S(1)}) custom-call(s32[8,128]{1,0:T(8,128)} %bitcast.5, s32[1,129]{1,0:T(1,128)} %bounds_hbm.1, f32[1]{0:T(128)} %bitcast.3.tau_hbm, bf16[64,4096]{1,0:T(8,128)(2,1)} %hid_hbm.1, ...), custom_call_target="tpu_custom_call" | custom-call | tf_op jit(solution)/shard_map/local_scores/pallas_call | solution.py:452
  8.6 32.4 %exchange.1 = (f32[2,64,128]{2,1,0:T(8,128)S(1)}, f32[64,128]{1,0:T(8,128)S(1)}) custom-call(f32[8,64,128]{2,1,0:T(8,128)S(1)} %get-tuple-element.11.score, bf16[1024,1024]{1,0:T(8,128)(2,1)S(1)} %get-tuple-element.12.dedup, f32[64,256]{1,0:T(8,128)S(1)} %get-tuple-element.13.logits, s32[3,4,40,128]{3,2,1,0:T(8,128)S(1)} %get-tuple-element.14.own_tab, ...), custom_call_target="tpu_custom_call" | custom-call | tf_op jit(solution)/shard_map/exchange/pallas_call | solution.py:472
  40.9 0.8 %mixture.1 = f32[64,256]{1,0:T(8,128)} custom-call(f32[2,64,128]{2,1,0:T(8,128)S(1)} %get-tuple-element.15.hist, f32[64,128]{1,0:T(8,128)S(1)} %get-tuple-element.16.stat, f32[64,256]{1,0:T(8,128)S(1)} %get-tuple-element.13.logits), custom_call_target="tpu_custom_call" | custom-call | tf_op jit(solution)/shard_map/mixture/pallas_call | solution.py:488

commit v8 on v7

--- a/solution.py
+++ b/solution.py
@@ -127,13 +127,13 @@
                 key_copy(2 * c + i + AHEAD).start()
 
         rows = pl.ds(c * 256, 256)
-        cross = lax.dot_general(hid[...], keys[rows, :], NT, preferred_element_type=F32)
+        cross = lax.dot_general(keys[rows, :], hid[...], NT, preferred_element_type=F32)
         sq = jnp.zeros((256, LN), F32)
         for t in range(keys.shape[1] // LN):
             k = keys[rows, t * LN:(t + 1) * LN].astype(F32)
             sq = sq + k * k
-        norm = jnp.sum(sq.T, axis=0, keepdims=True)
-        sc = (2.0 * cross - norm) / tau
+        norm = jnp.sum(sq, axis=1, keepdims=True)
+        sc = ((2.0 * cross - norm) / tau).T
         score[2 * c] = sc[:, :LN]
         score[2 * c + 1] = sc[:, LN:]
         return carry
@@ -298,19 +298,27 @@
             return own[g].at[core]
         return lists[g].at[2 * k - 1 + l]
 
+    smem_copies = []
+
+    def scalars(a, k, l):
+        c = pltpu.make_async_copy(tab_of(a, k, l).at[pl.ds(inner, 2)], tab_smem.at[a, k, l], smem_sem.at[a, k, l])
+        c.start()
+        smem_copies.append(c)
+
+    for a in range(3):
+        scalars(a, 0, 0)
     for d in near + far:
         for a in range(3):
             tab_copy(a, d).wait_recv()
             go(tab_share(a, d))
+            scalars(a, n - d, 0)
     tab_swap.wait_recv()
+    for a in range(3):
+        scalars(a, 0, 1)
     for d in near + far:
         for a in range(3):
             tab_share(a, d).wait_recv()
-    smem_copies = [pltpu.make_async_copy(tab_of(axis_of[g], k, l).at[pl.ds(inner, 2)], tab_smem.at[g, k, l],
-                                         smem_sem.at[g, k, l])
-                   for g in range(3) for k in range(n) for l in range(2)]
-    for c in smem_copies:
-        c.start()
+            scalars(a, n - d, 1)
     for c in smem_copies:
         c.wait()
 
@@ -332,7 +340,7 @@
             for i, (k, l) in enumerate(src):
                 packed = jnp.broadcast_to(tab_of(a, k, l)[pl.ds(row, 1), :], (nr, LN))
                 for hf in range(2):
-                    u = tab_smem[g, k, l, hf, ((n - k) % n) * inner + row]
+                    u = tab_smem[a, k, l, hf, ((n - k) % n) * inner + row]
                     kt = lax.shift_right_logical(u, 7)
                     merged = jnp.where(ln >= (u & 127), scaled[g][i, kt], scaled[g][i, kt + 1])
                     code = lax.shift_right_logical(packed, 8) if hf else packed

time: 41.8 us -> 41.4 us (level)
  no operation moved by 1% of the time
where the time goes in v8:
time: 41.4 us; the launch traced here: 41.3 us
  Pallas kernels  40 us (97%)
  between operations  1.31 us (3%)
    pallas_call x1, Pallas kernels, step(): pl.pallas_call(functools.partial(exchange_kernel, n), out_shape=(V((2, 64...  32.1 us
    pallas_call x1, Pallas kernels, step(): pl.pallas_call(functools.partial(local_kernel, n), out_shape=(V((8, 64, L...  7.1 us

profile of v8, /device:TPU:1, one launch (start us, length us, event | category | flops | bytes accessed | tf_op | source)
XLA Modules:
  0.0 41.3 jit_solution(17148556498508708569)
XLA Ops:
  1.3 7.1 %local_scores.1 = (f32[8,64,128]{2,1,0:T(8,128)S(1)}, bf16[1024,1024]{1,0:T(8,128)(2,1)S(1)}, f32[64,256]{1,0:T(8,128)S(1)}, s32[3,4,40,128]{3,2,1,0:T(8,128)S(1)}) custom-call(s32[8,128]{1,0:T(8,128)} %bitcast.5, s32[1,129]{1,0:T(1,128)} %bounds_hbm.1, f32[1]{0:T(128)} %bitcast.3.tau_hbm, bf16[64,4096]{1,0:T(8,128)(2,1)} %hid_hbm.1, ...), custom_call_target="tpu_custom_call" | custom-call | tf_op jit(solution)/shard_map/local_scores/pallas_call | solution.py:460
  8.4 32.1 %exchange.1 = (f32[2,64,128]{2,1,0:T(8,128)S(1)}, f32[64,128]{1,0:T(8,128)S(1)}) custom-call(f32[8,64,128]{2,1,0:T(8,128)S(1)} %get-tuple-element.11.score, bf16[1024,1024]{1,0:T(8,128)(2,1)S(1)} %get-tuple-element.12.dedup, f32[64,256]{1,0:T(8,128)S(1)} %get-tuple-element.13.logits, s32[3,4,40,128]{3,2,1,0:T(8,128)S(1)} %get-tuple-element.14.own_tab, ...), custom_call_target="tpu_custom_call" | custom-call | tf_op jit(solution)/shard_map/exchange/pallas_call | solution.py:480
  40.5 0.8 %mixture.1 = f32[64,256]{1,0:T(8,128)} custom-call(f32[2,64,128]{2,1,0:T(8,128)S(1)} %get-tuple-element.15.hist, f32[64,128]{1,0:T(8,128)S(1)} %get-tuple-element.16.stat, f32[64,256]{1,0:T(8,128)S(1)} %get-tuple-element.13.logits), custom_call_target="tpu_custom_call" | custom-call | tf_op jit(solution)/shard_map/mixture/pallas_call | solution.py:496

commit v9 on v8

--- a/solution.py
+++ b/solution.py
@@ -351,7 +351,7 @@
             part2[g][d2, t + 1] = acc[1]
             return carry
 
-        lax.fori_loop(0, mid, pair_step, 0, unroll=UNROLL)
+        lax.fori_loop(0, mid, pair_step, 0, unroll=UNROLL * (2 if d2 in far else 1))
 
     halves = (pl.ds(0, mid + 1), pl.ds(mid + 1, mid + 1))
     stat_at = (mid, 0)

time: 41.4 us -> 41.3 us (level)
  no operation moved by 1% of the time
where the time goes in v9:
time: 41.3 us; the launch traced here: 41.2 us
  Pallas kernels  39.9 us (97%)
  between operations  1.31 us (3%)
    pallas_call x1, Pallas kernels, step(): pl.pallas_call(functools.partial(exchange_kernel, n), out_shape=(V((2, 64...  32 us
    pallas_call x1, Pallas kernels, step(): pl.pallas_call(functools.partial(local_kernel, n), out_shape=(V((8, 64, L...  7.1 us

profile of v9, /device:TPU:1, one launch (start us, length us, event | category | flops | bytes accessed | tf_op | source)
XLA Modules:
  0.0 41.2 jit_solution(17082654778331333953)
XLA Ops:
  1.3 7.1 %local_scores.1 = (f32[8,64,128]{2,1,0:T(8,128)S(1)}, bf16[1024,1024]{1,0:T(8,128)(2,1)S(1)}, f32[64,256]{1,0:T(8,128)S(1)}, s32[3,4,40,128]{3,2,1,0:T(8,128)S(1)}) custom-call(s32[8,128]{1,0:T(8,128)} %bitcast.5, s32[1,129]{1,0:T(1,128)} %bounds_hbm.1, f32[1]{0:T(128)} %bitcast.3.tau_hbm, bf16[64,4096]{1,0:T(8,128)(2,1)} %hid_hbm.1, ...), custom_call_target="tpu_custom_call" | custom-call | tf_op jit(solution)/shard_map/local_scores/pallas_call | solution.py:460
  8.4 32.0 %exchange.1 = (f32[2,64,128]{2,1,0:T(8,128)S(1)}, f32[64,128]{1,0:T(8,128)S(1)}) custom-call(f32[8,64,128]{2,1,0:T(8,128)S(1)} %get-tuple-element.11.score, bf16[1024,1024]{1,0:T(8,128)(2,1)S(1)} %get-tuple-element.12.dedup, f32[64,256]{1,0:T(8,128)S(1)} %get-tuple-element.13.logits, s32[3,4,40,128]{3,2,1,0:T(8,128)S(1)} %get-tuple-element.14.own_tab, ...), custom_call_target="tpu_custom_call" | custom-call | tf_op jit(solution)/shard_map/exchange/pallas_call | solution.py:480
  40.4 0.8 %mixture.1 = f32[64,256]{1,0:T(8,128)} custom-call(f32[2,64,128]{2,1,0:T(8,128)S(1)} %get-tuple-element.15.hist, f32[64,128]{1,0:T(8,128)S(1)} %get-tuple-element.16.stat, f32[64,256]{1,0:T(8,128)S(1)} %get-tuple-element.13.logits), custom_call_target="tpu_custom_call" | custom-call | tf_op jit(solution)/shard_map/mixture/pallas_call | solution.py:496
